TPU v7x, 32 devices: a whole 2x2x4 slice. The times are simulated.
32 devices in a mesh: grp: 4 (over y, x), sp: 8 (over z, core).
Axes of the slice: x: 2, y: 2, z: 4, core: 2. Of those that a mesh axis runs over, the one named last changes fastest.
Arguments:
- layer_input: bfloat16 [8192, 768], P(('grp', 'sp')), may hold values from -6 to 6
- block_order: int32 [4, 16], P('grp'), may hold values from 0 to 15, each once within a row
- ln1_gain: float32 [768], replicated, may hold values from 0.5 to 1.5
- ln1_bias: float32 [768], replicated, may hold values from -1.8 to 1.8
- w_query: bfloat16 [768, 768], replicated, may hold values from -0.4375 to 0.4375
- b_query: float32 [768], replicated, may hold values from -1.8 to 1.8
- w_keyval: bfloat16 [768, 128], replicated, may hold values from -0.21875 to 0.21875
- b_keyval: float32 [128], replicated, may hold values from -1.8 to 1.8
- w_attn_out: bfloat16 [768, 768], replicated, may hold values from -0.875 to 0.875
- b_attn_out: float32 [768], replicated, may hold values from -1.8 to 1.8
- ln2_gain: float32 [768], replicated, may hold values from 0.5 to 1.5
- ln2_bias: float32 [768], replicated, may hold values from -1.8 to 1.8
- w_fc: bfloat16 [768, 3072], replicated, may hold values from -0.21875 to 0.21875
- b_fc: float32 [3072], replicated, may hold values from -1.8 to 1.8
- w_proj: bfloat16 [3072, 768], replicated, may hold values from -0.15625 to 0.15625
- b_proj: float32 [768], replicated, may hold values from -1.8 to 1.8
- kv_grad: bfloat16 [8192, 128], P(('grp', 'sp')), may hold values from -6 to 6
- out_grad: bfloat16 [8192, 768], P(('grp', 'sp')), may hold values from -16 to 16
Outputs:
- layer_out: bfloat16 [8192, 768], P(('grp', 'sp'))
- input_grad: float32 [8192, 768], P(('grp', 'sp'))
- ln1_gain_grad: float32 [768], replicated
- ln1_bias_grad: float32 [768], replicated
- w_query_grad: float32 [768, 768], P('sp')
- b_query_grad: float32 [768], replicated
- w_keyval_grad: float32 [768, 128], P('sp')
- b_keyval_grad: float32 [128], replicated
- w_attn_out_grad: float32 [768, 768], P('sp')
- b_attn_out_grad: float32 [768], replicated
- ln2_gain_grad: float32 [768], replicated
- ln2_bias_grad: float32 [768], replicated
- w_fc_grad: float32 [768, 3072], P('sp')
- b_fc_grad: float32 [3072], replicated
- w_proj_grad: float32 [3072, 768], P('sp')
- b_proj_grad: float32 [768], replicated
Inputs may be any that keep to these rules, and one draw needn't show every extreme that they name: `block_order`: each row names each of the 16 blocks of its sequence exactly once.
All inputs are finite; a program needn't handle non-finite values.
Results may differ from a plain program's by a relative error of at most 0.012.
The roundings to bfloat16 on the way count: a program that leaves them out, or rounds other values in their place, can miss the bound.
Values may be sent and summed in bfloat16 or wider, within the bound.
A program may use at most 128 MiB of HBM per device.

v0:
```python
import math

import jax
import jax.numpy as jnp
from jax import lax
from jax.sharding import PartitionSpec as P

H = 12
HD = 64
ROT = 16


norm_eps = 1e-05
half_root = 0.7071067811865476
inv_root_tau = 0.3989422804014327
masked_score = -1e30
rotary_base_log = math.log(10000.0)
score_block = 512


def layer_norm(values, gain_row, shift_row):
    centre = jnp.mean(values, axis=-1, keepdims=True)
    centred = values - centre
    spread = jnp.mean(centred * centred, axis=-1, keepdims=True)
    inverse_dev = lax.rsqrt(spread + norm_eps)
    normed = centred * inverse_dev
    return (normed * gain_row + shift_row, normed, inverse_dev)


def norm_back(upstream, normed, inverse_dev, gain_row):
    scaled = upstream * gain_row
    return inverse_dev * (
        scaled
        - jnp.mean(scaled, axis=-1, keepdims=True)
        - normed * jnp.mean(scaled * normed, axis=-1, keepdims=True)
    )


def rotary_tables(position):
    half_rot = ROT // 2
    frequency = jnp.exp(jnp.arange(half_rot, dtype=jnp.float32) * (-2.0 * rotary_base_log / ROT))
    angles = position.astype(jnp.float32)[:, None] * 0.25 * frequency[None, :]
    return (jnp.cos(angles), jnp.sin(angles))


def rotate(values, cosine, sine_table):
    half_rot = ROT // 2
    cos_rows = cosine[:, None, :]
    sin_rows = sine_table[:, None, :]
    lower_half = values[..., :half_rot]
    upper_half = values[..., half_rot:ROT]
    return jnp.concatenate(
        [
            lower_half * cos_rows - upper_half * sin_rows,
            upper_half * cos_rows + lower_half * sin_rows,
            values[..., ROT:],
        ],
        axis=-1,
    )


def rotate_back(values, cosine, sine_table):
    half_rot = ROT // 2
    cos_rows = cosine[:, None, :]
    sin_rows = sine_table[:, None, :]
    lower_half = values[..., :half_rot]
    upper_half = values[..., half_rot:ROT]
    return jnp.concatenate(
        [
            lower_half * cos_rows + upper_half * sin_rows,
            upper_half * cos_rows - lower_half * sin_rows,
            values[..., ROT:],
        ],
        axis=-1,
    )


def key_scores(query_rows, row_pos, kv_sequence, block_index, block_rows):
    key_start = block_index * block_rows
    key_slice = lax.dynamic_slice_in_dim(kv_sequence, key_start, block_rows, 0)
    raw_scores = (
        jnp.einsum("rd,kd->rk", query_rows, key_slice[:, :HD], preferred_element_type=jnp.float32)
        * 0.125
    )
    key_pos = key_start + lax.broadcasted_iota(jnp.int32, (1, block_rows), 1)
    return (jnp.where(key_pos <= row_pos[:, None], raw_scores, masked_score), key_slice)


def attention_forward(query_tiles, tile_pos, kv_sorted):
    pair_count = query_tiles.shape[0]
    pairs_per_seq = pair_count // kv_sorted.shape[0]
    block_rows = min(score_block, kv_sorted.shape[1])

    def one_pair(inputs):
        query_rows, row_pos, pair_index = inputs
        kv_sequence = kv_sorted[pair_index // pairs_per_seq]
        key_blocks = jnp.max(row_pos) // block_rows + 1
        row_count = query_rows.shape[0]

        def max_pass(block_index, carried):
            running_max, running_sum = carried
            masked, key_slice = key_scores(
                query_rows, row_pos, kv_sequence, block_index, block_rows
            )
            new_max = jnp.maximum(running_max, jnp.max(masked, axis=1, keepdims=True))
            running_sum = running_sum * jnp.exp(running_max - new_max) + jnp.sum(
                jnp.exp(masked - new_max), axis=1, keepdims=True
            )
            return (new_max, running_sum)

        start_max = jnp.full((row_count, 1), masked_score, jnp.float32)
        running_max, running_sum = lax.fori_loop(
            0, key_blocks, max_pass, (start_max, jnp.zeros((row_count, 1), jnp.float32))
        )
        log_total = running_max + jnp.log(running_sum)

        def value_pass(block_index, output):
            masked, key_slice = key_scores(
                query_rows, row_pos, kv_sequence, block_index, block_rows
            )
            weights = jnp.exp(masked - log_total).astype(jnp.bfloat16)
            return output + jnp.dot(weights, key_slice[:, HD:], preferred_element_type=jnp.float32)

        output = lax.fori_loop(0, key_blocks, value_pass, jnp.zeros((row_count, HD), jnp.float32))
        return (output, log_total)

    return lax.map(one_pair, (query_tiles, tile_pos, jnp.arange(pair_count, dtype=jnp.int32)))


def attention_backward(query_tiles, tile_pos, grad_tiles, log_totals, kv_sorted):
    pair_count = query_tiles.shape[0]
    pairs_per_seq = pair_count // kv_sorted.shape[0]
    block_rows = min(score_block, kv_sorted.shape[1])
    pair_width = kv_sorted.shape[2]

    def one_pair(key_grads, inputs):
        query_rows, row_pos, grad_rows, log_total, pair_index = inputs
        sequence = pair_index // pairs_per_seq
        kv_sequence = kv_sorted[sequence]
        key_blocks = jnp.max(row_pos) // block_rows + 1
        row_count = query_rows.shape[0]

        def pass_terms(block_index):
            masked, key_slice = key_scores(
                query_rows, row_pos, kv_sequence, block_index, block_rows
            )
            weights = jnp.exp(masked - log_total)
            weight_grads = jnp.einsum(
                "rd,kd->rk", grad_rows, key_slice[:, HD:], preferred_element_type=jnp.float32
            )
            return (weights, weight_grads, key_slice)

        def delta_pass(block_index, row_delta):
            weights, weight_grads, unused_slice = pass_terms(block_index)
            return row_delta + jnp.sum(weights * weight_grads, axis=1, keepdims=True)

        row_delta = lax.fori_loop(0, key_blocks, delta_pass, jnp.zeros((row_count, 1), jnp.float32))

        def grad_pass(block_index, carried):
            query_grad, sequence_grads = carried
            weights, weight_grads, key_slice = pass_terms(block_index)
            score_grad = (weights * (weight_grads - row_delta)).astype(jnp.bfloat16)
            query_grad = (
                query_grad
                + jnp.dot(score_grad, key_slice[:, :HD], preferred_element_type=jnp.float32) * 0.125
            )
            key_part = (
                jnp.einsum("rk,rd->kd", score_grad, query_rows, preferred_element_type=jnp.float32)
                * 0.125
            )
            value_part = jnp.einsum(
                "rk,rd->kd",
                weights.astype(jnp.bfloat16),
                grad_rows,
                preferred_element_type=jnp.float32,
            )
            key_start = block_index * block_rows
            previous = lax.dynamic_slice(
                sequence_grads, (sequence, key_start, 0), (1, block_rows, pair_width)
            )
            updated = previous + jnp.concatenate([key_part, value_part], axis=1)[None]
            return (
                query_grad,
                lax.dynamic_update_slice(sequence_grads, updated, (sequence, key_start, 0)),
            )

        query_grad, key_grads = lax.fori_loop(
            0, key_blocks, grad_pass, (jnp.zeros((row_count, HD), jnp.float32), key_grads)
        )
        return (key_grads, query_grad)

    start_grads = jnp.zeros(kv_sorted.shape, jnp.float32)
    key_grads, query_grads = lax.scan(
        one_pair,
        start_grads,
        (query_tiles, tile_pos, grad_tiles, log_totals, jnp.arange(pair_count, dtype=jnp.int32)),
    )
    return (query_grads, key_grads)


def local(
    layer_input,
    block_order,
    ln1_gain,
    ln1_bias,
    w_query,
    b_query,
    w_keyval,
    b_keyval,
    w_attn_out,
    b_attn_out,
    ln2_gain,
    ln2_bias,
    w_fc,
    b_fc,
    w_proj,
    b_proj,
    kv_grad,
    out_grad,
):
    my_rank = lax.axis_index("sp")
    seq_count = block_order.shape[0]
    block_count = block_order.shape[1]
    token_count = layer_input.shape[0]
    shard_len = token_count // seq_count
    block_len = shard_len // 2
    model_width = layer_input.shape[1]
    pair_width = 2 * HD
    pair_count = 2 * seq_count
    input_float = layer_input.astype(jnp.float32)
    first_in, first_hat, first_inv = layer_norm(input_float, ln1_gain, ln1_bias)
    first_low = first_in.astype(jnp.bfloat16)
    query_pre = jnp.dot(first_low, w_query, preferred_element_type=jnp.float32) + b_query
    keyval_pre = jnp.dot(first_low, w_keyval, preferred_element_type=jnp.float32) + b_keyval
    offsets = jnp.arange(block_len, dtype=jnp.int32)
    own_blocks = lax.dynamic_slice_in_dim(block_order, 2 * my_rank, 2, 1)
    own_pos = (own_blocks[:, :, None] * block_len + offsets[None, None, :]).reshape(token_count)
    cosine, sine_table = rotary_tables(own_pos)
    query_use = (
        rotate(query_pre.reshape(token_count, H, HD), cosine, sine_table)
        .reshape(token_count, model_width)
        .astype(jnp.bfloat16)
    )
    key_rot = rotate(keyval_pre[:, None, :HD], cosine, sine_table)[:, 0, :]
    keyval_use = jnp.concatenate([key_rot, keyval_pre[:, HD:]], axis=1).astype(jnp.bfloat16)
    gathered = lax.all_gather(
        keyval_use.reshape(seq_count, shard_len, pair_width), "sp", axis=1, tiled=True
    )
    seq_len = gathered.shape[1]
    block_sorter = jnp.argsort(block_order, axis=1)
    kv_sorted = jnp.take_along_axis(
        gathered.reshape(seq_count, block_count, block_len, pair_width),
        block_sorter[:, :, None, None],
        axis=1,
    ).reshape(seq_count, seq_len, pair_width)
    row_pos = own_pos.reshape(seq_count, shard_len)
    query_rows = query_use.reshape(seq_count, shard_len, model_width)
    query_tiles = query_rows.reshape(pair_count, block_len * H, HD)
    tile_pos = jnp.repeat(row_pos.reshape(pair_count, block_len), H, axis=1)
    head_rows, log_totals = attention_forward(query_tiles, tile_pos, kv_sorted)
    heads_sorted = head_rows.reshape(seq_count, shard_len, model_width).astype(jnp.bfloat16)
    heads_local = heads_sorted.reshape(token_count, model_width)
    attn_branch = jnp.dot(heads_local, w_attn_out, preferred_element_type=jnp.float32) + b_attn_out
    second_in, second_hat, second_inv = layer_norm(input_float, ln2_gain, ln2_bias)
    second_low = second_in.astype(jnp.bfloat16)
    hidden = jnp.dot(second_low, w_fc, preferred_element_type=jnp.float32) + b_fc
    erf_part = 1.0 + lax.erf(hidden * half_root)
    activated = (0.5 * hidden * erf_part).astype(jnp.bfloat16)
    mlp_branch = jnp.dot(activated, w_proj, preferred_element_type=jnp.float32) + b_proj
    layer_out = (input_float + attn_branch + mlp_branch).astype(jnp.bfloat16)
    upstream = out_grad.astype(jnp.float32)
    column_sum = jnp.sum(upstream, axis=0)
    w_proj_grad = jnp.einsum("tf,td->fd", activated, out_grad, preferred_element_type=jnp.float32)
    act_grad = jnp.einsum("td,fd->tf", out_grad, w_proj, preferred_element_type=jnp.float32)
    gelu_slope = 0.5 * erf_part + hidden * jnp.exp(-0.5 * hidden * hidden) * inv_root_tau
    hidden_grad = (act_grad * gelu_slope).astype(jnp.bfloat16)
    w_fc_grad = jnp.einsum("td,tf->df", second_low, hidden_grad, preferred_element_type=jnp.float32)
    b_fc_grad = jnp.sum(hidden_grad.astype(jnp.float32), axis=0)
    second_grad = jnp.einsum("tf,df->td", hidden_grad, w_fc, preferred_element_type=jnp.float32)
    w_attn_out_grad = jnp.einsum(
        "te,td->ed", heads_local, out_grad, preferred_element_type=jnp.float32
    )
    heads_grad = jnp.einsum(
        "td,ed->te", out_grad, w_attn_out, preferred_element_type=jnp.float32
    ).astype(jnp.bfloat16)
    grad_rows = heads_grad.reshape(seq_count, shard_len, model_width)
    grad_tiles = grad_rows.reshape(pair_count, block_len * H, HD)
    query_tile_grads, sorted_kv_grads = attention_backward(
        query_tiles, tile_pos, grad_tiles, log_totals, kv_sorted
    )
    query_rot_rows = query_tile_grads.reshape(seq_count, shard_len, model_width)
    query_rot_grad = query_rot_rows.reshape(token_count, model_width)
    query_grad = (
        rotate_back(query_rot_grad.reshape(token_count, H, HD), cosine, sine_table)
        .reshape(token_count, model_width)
        .astype(jnp.bfloat16)
    )
    stored_kv_grads = jnp.take_along_axis(
        sorted_kv_grads.reshape(seq_count, block_count, block_len, pair_width),
        block_order[:, :, None, None],
        axis=1,
    ).reshape(seq_count, seq_len, pair_width)
    own_kv_grad = lax.psum_scatter(stored_kv_grads, "sp", scatter_dimension=1, tiled=True).reshape(
        token_count, pair_width
    ) + kv_grad.astype(jnp.float32)
    key_pre_grad = rotate_back(own_kv_grad[:, None, :HD], cosine, sine_table)[:, 0, :]
    keyval_grad = jnp.concatenate([key_pre_grad, own_kv_grad[:, HD:]], axis=1).astype(jnp.bfloat16)
    w_query_grad = jnp.einsum(
        "td,te->de", first_low, query_grad, preferred_element_type=jnp.float32
    )
    b_query_grad = jnp.sum(query_grad.astype(jnp.float32), axis=0)
    w_keyval_grad = jnp.einsum(
        "td,te->de", first_low, keyval_grad, preferred_element_type=jnp.float32
    )
    b_keyval_grad = jnp.sum(keyval_grad.astype(jnp.float32), axis=0)
    first_grad = jnp.einsum(
        "te,de->td", query_grad, w_query, preferred_element_type=jnp.float32
    ) + jnp.einsum("te,de->td", keyval_grad, w_keyval, preferred_element_type=jnp.float32)
    first_back = norm_back(first_grad, first_hat, first_inv, ln1_gain)
    second_back = norm_back(second_grad, second_hat, second_inv, ln2_gain)
    input_grad = upstream + first_back + second_back
    (
        ln1_gain_grad,
        ln1_bias_grad,
        b_query_total,
        b_keyval_total,
        bias_out_total,
        ln2_gain_grad,
        ln2_bias_grad,
        b_fc_total,
    ) = lax.psum(
        (
            jnp.sum(first_grad * first_hat, axis=0),
            jnp.sum(first_grad, axis=0),
            b_query_grad,
            b_keyval_grad,
            column_sum,
            jnp.sum(second_grad * second_hat, axis=0),
            jnp.sum(second_grad, axis=0),
            b_fc_grad,
        ),
        ("grp", "sp"),
    )
    query_share, keyval_share, out_share, fc_share, proj_share = (
        lax.psum_scatter(w_query_grad, "sp", scatter_dimension=0, tiled=True),
        lax.psum_scatter(w_keyval_grad, "sp", scatter_dimension=0, tiled=True),
        lax.psum_scatter(w_attn_out_grad, "sp", scatter_dimension=0, tiled=True),
        lax.psum_scatter(w_fc_grad, "sp", scatter_dimension=0, tiled=True),
        lax.psum_scatter(w_proj_grad, "sp", scatter_dimension=0, tiled=True),
    )
    query_total, keyval_total, out_total, fc_total, proj_total = lax.psum(
        (query_share, keyval_share, out_share, fc_share, proj_share), "grp"
    )
    return (
        layer_out,
        input_grad,
        ln1_gain_grad,
        ln1_bias_grad,
        query_total,
        b_query_total,
        keyval_total,
        b_keyval_total,
        out_total,
        bias_out_total,
        ln2_gain_grad,
        ln2_bias_grad,
        fc_total,
        b_fc_total,
        proj_total,
        bias_out_total,
    )


def solution(mesh):
    placed = (
        P(("grp", "sp"), None),
        P("grp", None),
        P(),
        P(),
        P(),
        P(),
        P(),
        P(),
        P(),
        P(),
        P(),
        P(),
        P(),
        P(),
        P(),
        P(),
        P(("grp", "sp"), None),
        P(("grp", "sp"), None),
    )
    return jax.shard_map(
        local,
        mesh=mesh,
        in_specs=placed,
        out_specs=(
            P(("grp", "sp"), None),
            P(("grp", "sp"), None),
            P(),
            P(),
            P("sp", None),
            P(),
            P("sp", None),
            P(),
            P("sp", None),
            P(),
            P(),
            P(),
            P("sp", None),
            P(),
            P("sp", None),
            P(),
        ),
        check_vma=False,
    )
```

profile of v0, /device:TPU:0, one launch (start us, length us, event | category | flops | bytes accessed | tf_op | source)
XLA Modules:
  0.0 592.1 jit_solution(3566352202850660433)
XLA Ops:
  30.8 16.7 %all_gather.3 = bf16[1,2048,128]{1,2,0:T(8,128)(2,1)S(1)} all-gather(bf16[1,256,128]{1,2,0:T(8,128)(2,1)S(1)} %pad_maximum_fusion.1), channel_id=1, replica_groups=mesh['grp'=4,'sp'=8] {'sp'}, dimensions={1}, use_global_device_ids=true | all-gather | bytes 589824 | tf_op jit(solution)/shard_map/all_gather | solution.py:246
  54.8 20.9 %while.137 = (s32[]{:T(128)}, bf16[2,1536,64]{1,2,0:T(8,128)(2,1)S(1)}, f32[2,1536,1]{1,2,0:T(1,128)S(1)}, s32[2,1536]{1,0:T(2,128)S(1)}, bf16[1,2048,128]{2,1,0...) while((s32[]{:T(128)}, ...), condition=%wide.region_11.12_spmd.clone, body=%wide.region_3.11_spmd.sunk.clone | while | flops 310746144 | bytes 10013081 | solution.py:127
  66.0 4.8 while.135
  70.8 4.8 while.136
  76.8 44.3 %while.140 = (s32[]{:T(128)}, f32[1,2048,128]{1,2,0:T(8,128)}, f32[2,1536,64]{1,2,0:T(8,128)}, s32[2,1536]{1,0:T(2,128)S(1)}, bf16[1,2048,128]{2,1,0:T(8,128)(2,...) while((s32[]{:T(128)}, f32[1,2048,128]{1,2,0:T(8,128)}, ...), condition=%wide.region_19.20_spmd.clone, body=%wide.region_12.19_spmd.sunk.clone | while | flops 716016128 | bytes 27012140 | solution.py:193
  83.1 5.0 while.139
  93.3 7.2 %while.138 = (s32[]{:T(128)}, f32[1536,1]{0,1:T(1,128)S(1)}, s32[]{:T(128)}, s32[1536]{0:T(1024)S(1)}, bf16[2048,128]{1,0:T(8,128)(2,1)S(1)}, /*index=5*/bf16[15...) while((s32[]{:T(128)}, f32[1536,1]{0,1:T(1,128)S(1)}, ...), condition=%wide.region_16.16_spmd, body=%wide.region_14.15_spmd.sunk | while | flops 206045696 | bytes 7397587 | solution.py:157
  100.5 19.8 %while.139 = (s32[]{:T(128)}, f32[1536,64]{0,1:T(8,128)S(1)}, f32[1,2048,128]{1,2,0:T(8,128)}, s32[]{:T(128)}, s32[1536]{0:T(1024)S(1)}, /*index=5*/bf16[2048,12...) while((s32[]{:T(128)}, f32[1536,64]{0,1:T(8,128)S(1)}, ...), condition=%wide.region_18.18_spmd, body=%wide.region_17.17_spmd.sunk | while | flops 509968896 | bytes 17617136 | solution.py:187
  129.6 2.5 copy.72
  132.1 2.6 fusion.108
  145.4 5.3 multiply_convert_fusion
  150.7 4.3 convert_reduce_fusion
  156.2 5.2 fusion.98
  161.5 6.5 %fusion.112 = f32[3072,768]{1,0:T(8,128)} fusion(bf16[256,3072]{1,0:T(8,128)(2,1)} %get-tuple-element.614, bf16[256,768]{1,0:T(8,128)(2,1)S(1)} %copy-done.4), kind=kOutput, calls=%fused_computation.201 | convolution fusion | flops 1207959552 | bytes 11403264 | tf_op jit(solution)/shard_map/tf,td->fd/dot_general | solution.py:273
  168.9 13.4 %reduce-scatter.7.cloned.1.call-done = f32[1,256,128]{1,2,0:T(8,128)} async-done(((f32[1,2048,128]{1,2,0:T(8,128)}), f32[1,256,128]{1,2,0:T(8,128)}) %reduce-scatter.7.cloned.1.call-update) | async-done | bytes 131088 | tf_op jit(solution)/shard_map/reduce_scatter | solution.py:303
  184.8 35.2 %reduce-scatter.9.cloned.1.call-done = f32[96,768]{1,0:T(8,128)} async-done(((f32[768,768]{1,0:T(8,128)}), f32[96,768]{1,0:T(8,128)}) %reduce-scatter.9.cloned.1.call-update) | async-done | bytes 294928 | tf_op jit(solution)/shard_map/reduce_scatter | solution.py:345
  220.0 38.3 %reduce-scatter.13.cloned.1.call-done = f32[96,768]{1,0:T(8,128)} async-done(((f32[768,768]{1,0:T(8,128)}), f32[96,768]{1,0:T(8,128)}) %reduce-scatter.13.cloned.1.call-update) | async-done | bytes 294928 | tf_op jit(solution)/shard_map/reduce_scatter | solution.py:347
  258.3 100.5 %reduce-scatter.15.cloned.1.call-done = f32[96,3072]{1,0:T(8,128)} async-done(((f32[768,3072]{1,0:T(8,128)}), f32[96,3072]{1,0:T(8,128)}) %reduce-scatter.15.cloned.1.call-update) | async-done | bytes 1179664 | tf_op jit(solution)/shard_map/reduce_scatter | solution.py:348
  358.8 100.1 %reduce-scatter.17.cloned.1.call-done = f32[384,768]{1,0:T(8,128)} async-done(((f32[3072,768]{1,0:T(8,128)}), f32[384,768]{1,0:T(8,128)}) %reduce-scatter.17.cloned.1.call-update) | async-done | bytes 1179664 | tf_op jit(solution)/shard_map/reduce_scatter | solution.py:349
  459.6 4.5 convolution_add_fusion.5
  469.4 39.5 %all-reduce = (f32[768]{0:T(1024)}, f32[768]{0:T(1024)}, f32[768]{0:T(1024)}, f32[128]{0:T(128)}, f32[768]{0:T(1024)S(1)}, /*index=5*/f32[768]{0:T(1024)}, f32[768]{0:T(1024)}, f32[3072]{0:T(1024)}) all-reduce(f32[768]{0:T(1024)S(1)} %get-tuple-element.476, ...), channel_id=1, replica_groups=mesh['grp'=4,'sp'=8] {'grp','sp'}, use_global_device_ids=true, to_apply=%region_26.27 | all-reduce | flops 7808 | bytes 62464 | tf_op jit(solution)/shard_map/psum | solution.py:331
  508.9 18.4 %psum.95 = f32[96,128]{1,0:T(8,128)} all-reduce(f32[96,128]{1,0:T(8,128)} %reduce-scatter.11.cloned.1.call-done), channel_id=1, replica_groups=mesh['grp'=4,'sp'=8] {'grp'}, use_global_device_ids=true, to_apply=%region_34.35 | all-reduce | flops 12288 | bytes 98304 | tf_op jit(solution)/shard_map/psum | solution.py:351
  527.3 50.6 %all-reduce.4.cloned.1.call-done = (f32[96,768]{1,0:T(8,128)}, f32[96,768]{1,0:T(8,128)}, f32[96,3072]{1,0:T(8,128)}, f32[384,768]{1,0:T(8,128)}) async-done(((f32[96,768]{1,0:T(8,128)}, f32[96,768]{1,0:T(8,128)}, f32[96,3072]{1,0:T(8,128)}, f32[384,768]{1,0:T(8,128)}), (f32[96,768]{1,0:T(8,128)}, f32[96,768]{1,0:T(8,128)}, f32[96,3072]{1,0:T(8,128)}, f32[384,768]{1,0:T(8,128)})) %all-reduce.4.cloned.1.call-update) | async-done | bytes 2949136 | tf_op jit(solution)/shard_map/psum | solution.py:351
  581.9 2.4 copy.144
  (331 shorter events, 123.7 us)
Async XLA Ops:
  7.2 40.6 %copy-start = (bf16[768,768]{1,0:T(8,128)(2,1)S(1)}, bf16[768,768]{1,0:T(8,128)(2,1)}, u32[]{:S(2)}) copy-start(bf16[768,768]{1,0:T(8,128)(2,1)} %param.34) | copy-start | bytes 3538948
  7.2 18.5 %copy-start.3 = (bf16[256,768]{1,0:T(8,128)(2,1)S(1)}, bf16[256,768]{1,0:T(8,128)(2,1)}, u32[]{:S(2)}) copy-start(bf16[256,768]{1,0:T(8,128)(2,1)} %param.47) | copy-start | bytes 1179652
  7.2 18.5 %copy-start.5 = (bf16[768,768]{1,0:T(8,128)(2,1)S(1)}, bf16[768,768]{1,0:T(8,128)(2,1)}, u32[]{:S(2)}) copy-start(bf16[768,768]{1,0:T(8,128)(2,1)} %param.38) | copy-start | bytes 3538948
  7.2 175.1 %reduce-scatter.7.cloned.1.call-start = ((), (), s32[]{:S(2)}) async-start(), calls=%async_computation.6 | async-start | bytes 1179648 | tf_op jit(solution)/shard_map/reduce_scatter | solution.py:303
  7.3 11.5 %copy-start.33 = (f32[8]{0:T(128)}, f32[8]{0:T(128)S(1)}, u32[]{:S(2)}) copy-start(f32[8]{0:T(128)S(1)} %multiply_exponential_fusion) | copy-start | bytes 100
  13.0 34.7 %copy-start.22 = (f32[256]{0:T(256)}, f32[256]{0:T(256)S(1)}, u32[]{:S(2)}) copy-start(f32[256]{0:T(256)S(1)} %broadcast_multiply_fusion.4) | copy-start | bytes 3076
  15.8 31.9 %copy-start.1 = (bf16[256,768]{1,0:T(8,128)(2,1)S(1)}, bf16[256,768]{1,0:T(8,128)(2,1)}, u32[]{:S(2)}) copy-start(bf16[256,768]{1,0:T(8,128)(2,1)} %param.30) | copy-start | bytes 1179652
  124.9 95.1 %reduce-scatter.9.cloned.1.call-start = ((), (), s32[]{:S(2)}) async-start(), calls=%async_computation.7 | async-start | bytes 2654208 | tf_op jit(solution)/shard_map/reduce_scatter | solution.py:345
  134.7 5.5 copy-start.2
  142.3 116.0 %reduce-scatter.13.cloned.1.call-start = ((), (), s32[]{:S(2)}) async-start(), calls=%async_computation.9 | async-start | bytes 2654208 | tf_op jit(solution)/shard_map/reduce_scatter | solution.py:347
  145.3 213.6 %reduce-scatter.15.cloned.1.call-start = ((), (), s32[]{:S(2)}) async-start(), calls=%async_computation.10 | async-start | bytes 10616832 | tf_op jit(solution)/shard_map/reduce_scatter | solution.py:348
  161.4 297.5 %reduce-scatter.17.cloned.1.call-start = ((), (), s32[]{:S(2)}) async-start(), calls=%async_computation.11 | async-start | bytes 10616832 | tf_op jit(solution)/shard_map/reduce_scatter | solution.py:349
  168.0 15.3 %copy-start.30 = (f32[256]{0:T(256)S(1)}, f32[256]{0:T(256)}, u32[]{:S(2)}) copy-start(f32[256]{0:T(256)} %copy-done.29) | copy-start | bytes 3076
  168.0 15.4 %copy-start.34 = (f32[8]{0:T(128)S(1)}, f32[8]{0:T(128)}, u32[]{:S(2)}) copy-start(f32[8]{0:T(128)} %copy-done.33) | copy-start | bytes 100
  168.0 15.5 %copy-start.28 = (f32[768]{0:T(1024)S(1)}, f32[768]{0:T(1024)}, u32[]{:S(2)}) copy-start(f32[768]{0:T(1024)} %param.32) | copy-start | bytes 9220
  168.0 15.5 %copy-start.36 = (f32[768]{0:T(1024)S(1)}, f32[768]{0:T(1024)}, u32[]{:S(2)}) copy-start(f32[768]{0:T(1024)} %param.33) | copy-start | bytes 9220
  168.0 291.0 %copy-start.24 = (f32[12,64]{1,0:T(8,128)S(1)}, f32[12,64]{1,0:T(8,128)}, u32[]{:S(2)}) copy-start(f32[12,64]{1,0:T(8,128)} %get-tuple-element.594) | copy-start | bytes 9220
  168.0 340.9 %reduce-scatter.11.cloned.1.call-start = ((), (), s32[]{:S(2)}) async-start(), calls=%async_computation.8 | async-start | bytes 442368 | tf_op jit(solution)/shard_map/reduce_scatter | solution.py:346
  184.7 274.9 %copy-start.41 = (f32[768]{0:T(1024)S(1)}, f32[768]{0:T(1024)}, u32[]{:S(2)}) copy-start(f32[768]{0:T(1024)} %param.45) | copy-start | bytes 9220
  184.7 393.2 %all-reduce.4.cloned.1.call-start = ((), (), s32[]{:S(2)}) async-start(), calls=%async_computation.12 | async-start | bytes 5898240 | tf_op jit(solution)/shard_map/psum | solution.py:351
  459.1 6.4 %slice-start = ((s8[4718592]{0:T(1024)(128)(4,1)}), s8[4194304]{0:T(1024)(128)(4,1)S(1)}, s32[]{:S(2)}) async-start(s8[4718592]{0:T(1024)(128)(4,1)} %bitcast.210), calls=%async_computation.13 | async-start | bytes 8388608
  459.6 5.9 slice-start.1
  508.9 76.4 %copy-start.38 = (f32[768]{0:T(1024)}, f32[768]{0:T(1024)S(1)}, u32[]{:S(2)}) copy-start(f32[768]{0:T(1024)S(1)} %get-tuple-element.1439) | copy-start | bytes 9220
  577.9 6.3 %copy-start.11 = (f32[384,768]{1,0:T(8,128)S(1)}, f32[384,768]{1,0:T(8,128)}, u32[]{:S(2)}) copy-start(f32[384,768]{1,0:T(8,128)} %get-tuple-element.1444) | copy-start | bytes 3538948
  (27 other events, 82.9 us)
Sparse Core Ops, SparseCore 0:
  125.0 57.3 reduce-scatter.6
  184.7 35.2 reduce-scatter.8
  222.3 35.9 reduce-scatter.12
  260.5 98.3 reduce-scatter.14
  361.0 97.9 reduce-scatter.16
  461.6 29.5 reduce-scatter.10
  494.7 83.1 all-reduce.3
where the time goes:
time: 595 us; the launch traced here: 592 us
  waiting for transfers between devices  338 us (57%)
  blocking collectives  74.6 us (13%)
  matrix products  73 us (12%)
  local copies, waits for them, and re-layouts  47.9 us (8%)
  other arithmetic  31.1 us (5%)
  between operations  14.8 us (2%)
  loops' own time  11.6 us (2%)
    reduce_scatter x1, waiting for transfers between devices, local(): lax.psum_scatter(w_fc_grad, 'sp', scatter_dimension=0, tiled=True)  101 us
    reduce_scatter x1, waiting for transfers between devices, local(): lax.psum_scatter(w_proj_grad, 'sp', scatter_dimension=0, tiled=True)  100 us
    psum x1, waiting for transfers between devices, local(): lax.psum((query_share, keyval_share, out_share, fc_share, proj_share), 'g...  50.6 us
    psum x1, blocking collectives, local(): lax.psum((jnp.sum(first_grad * first_hat, axis=0), jnp.sum(first_grad, ax...  39.5 us
    reduce_scatter x1, waiting for transfers between devices, local(): lax.psum_scatter(w_attn_out_grad, 'sp', scatter_dimension=0, tiled=True)  38.3 us
    reduce_scatter x1, waiting for transfers between devices, local(): lax.psum_scatter(w_query_grad, 'sp', scatter_dimension=0, tiled=True)  35.2 us
    psum x1, blocking collectives, local(): lax.psum((query_share, keyval_share, out_share, fc_share, proj_share), 'g...  18.4 us
    all_gather x1, blocking collectives, local(): lax.all_gather(keyval_use.reshape(seq_count, shard_len, pair_width), 'sp'...  16.7 us
  transfers between devices with their start and end apart: 7, of which 6 were waited for; matrix products, arithmetic and copies ran while one was open for 9% of the time, Pallas kernels for 0%

commit v1 on v0

--- a/solution.py
+++ b/solution.py
@@ -1,14 +1,26 @@
+import functools
 import math
 
 import jax
 import jax.numpy as jnp
 from jax import lax
+from jax.experimental import pallas as pl
+from jax.experimental.pallas import tpu as pltpu
 from jax.sharding import PartitionSpec as P
 
 H = 12
 HD = 64
 ROT = 16
-
+MESH = pl.DeviceIdType.MESH
+F32 = jnp.float32
+BF16 = jnp.bfloat16
+NN = (((1,), (0,)), ((), ()))
+NT = (((1,), (1,)), ((), ()))
+TN = (((0,), (0,)), ((), ()))
+
+
+def mm(a, b, dims=NN):
+    return lax.dot_general(a, b, dims, preferred_element_type=F32)
 
 norm_eps = 1e-05
 half_root = 0.7071067811865476
@@ -16,6 +28,874 @@
 masked_score = -1e30
 rotary_base_log = math.log(10000.0)
 score_block = 512
+
+
+def vec_rows(width, ff, pair):
+    names = ("ln1_gain", "ln1_bias", "b_query", "b_keyval", "column", "ln2_gain", "ln2_bias", "b_fc")
+    sizes = (width, width, width, pair, width, width, width, ff)
+    at, rows = 0, {}
+    for name, size in zip(names, sizes):
+        rows[name] = (at, size // 128)
+        at += size // 128
+    return rows, at
+
+
+def fused_kernel(
+    dims,
+    x_h,
+    order_s,
+    g1_h,
+    b1_h,
+    wq_h,
+    bq_h,
+    wkv_h,
+    bkv_h,
+    wo_h,
+    bo_h,
+    g2_h,
+    b2_h,
+    wfc_h,
+    bfc_h,
+    wpr_h,
+    bpr_h,
+    kvg_h,
+    og_h,
+    o_wp,
+    o_wf,
+    o_wo,
+    o_wq,
+    o_wkv,
+    o_vec,
+    o_lo,
+    o_ig,
+    vecs,
+    bkv_v,
+    bfc_v,
+    x2,
+    og2,
+    fi2,
+    si2,
+    fit,
+    sit,
+    nrm,
+    inv,
+    wkv_v,
+    wq_v,
+    wo_v,
+    wfc_v,
+    wpr_v,
+    kvg_v,
+    act_s,
+    hg_s,
+    mlp_all,
+    sec_all,
+    mlp_r,
+    sec_r,
+    wp_part,
+    rx_wp,
+    wp_s1,
+    ry_wp,
+    zs_wp,
+    rz_wp,
+    fin_wp,
+    wf_part,
+    ry_wf,
+    wf_s1,
+    wf_own,
+    rx_wf,
+    zs_wf,
+    rz_wf,
+    fin_wf,
+    kv_all,
+    kvt,
+    qo,
+    bias,
+    sbuf,
+    dbuf,
+    dsp,
+    dkv,
+    dkv_b,
+    rdkv,
+    oht,
+    qgt,
+    ht_r,
+    qg2,
+    wo_part,
+    rx_wo,
+    wo_s1,
+    ry_wo,
+    zs_wo,
+    rz_wo,
+    fin_wo,
+    wq_part,
+    ry_wq,
+    wq_s1,
+    rx_wq,
+    zs_wq,
+    rz_wq,
+    fin_wq,
+    vec,
+    rvec,
+    wkv_part,
+    wkv_b,
+    rkv,
+    sm,
+    fin_kv,
+    fin_vec,
+    lo_v,
+    ig_v,
+    ctab,
+    stab,
+    cost,
+    sint,
+    lsem,
+    ssem,
+    rsem,
+):
+    T, D, F, S, NSP, NG = dims
+    NZ = NSP // 2
+    Q = F // NSP
+    R = D // NSP
+    C2 = D // 2
+    pair = 2 * HD
+    g = lax.axis_index("grp")
+    d = lax.axis_index("sp")
+    c = lax.rem(d, 2)
+    z = lax.div(d, 2)
+    xx = lax.rem(g, 2)
+    yy = lax.div(g, 2)
+    partner = (g, d + 1 - 2 * c)
+    xnb = (g + 1 - 2 * xx, d)
+    ynb = (g + 2 - 4 * yy, d)
+
+    def sp_peer(o):
+        return (g, lax.rem(d + o, NSP))
+
+    def z_peer(o):
+        return (g, 2 * lax.rem(z + o, NZ) + c)
+
+    def xy_peer(o, core):
+        return (lax.rem(g + o, NG), 2 * z + core)
+
+    base = {}
+    used = [0]
+
+    def take(name, n):
+        base[name] = used[0]
+        used[0] += n
+
+    for name, n in (
+        ("x", 1), ("og", 1), ("kv", NSP), ("mlp", 1), ("sec", 1),
+        ("wpx", NZ), ("wpy", NZ), ("wpz", NZ), ("wpg", NG),
+        ("wfy", 2), ("wfx", 1), ("wfz", NZ), ("wfg", 2 * NG),
+        ("ht", NZ), ("qg", 1), ("dkv", NSP),
+        ("wox", 1), ("woy", 1), ("woz", NZ), ("wog", NG),
+        ("wqy", 1), ("wqx", 1), ("wqz", NZ), ("wqg", NG),
+        ("wkv", NSP), ("vec", NSP), ("sm", NG), ("vg", NSP),
+    ):
+        take(name, n)
+
+    def rc(name, i, src, dst, to):
+        k = base[name] + i
+        return pltpu.make_async_remote_copy(
+            src_ref=src,
+            dst_ref=dst,
+            send_sem=ssem.at[k],
+            recv_sem=rsem.at[k],
+            device_id=to,
+            device_id_type=MESH,
+        )
+
+    started = []
+
+    def send(copy):
+        copy.start()
+        started.append(copy)
+
+    lused = [0]
+
+    def lc(src, dst):
+        copy = pltpu.make_async_copy(src, dst, lsem.at[lused[0]])
+        lused[0] += 1
+        copy.start()
+        return copy
+
+    def chunk_of(j):
+        far_y = lax.div(j, 2) == 0
+        far_x = lax.rem(j, 2) == 0
+        return 2 * jnp.where(far_y, 1 - yy, yy) + jnp.where(far_x, 1 - xx, xx)
+
+    def chunk_in(j):
+        far_y = lax.div(j, 2) == 0
+        far_x = lax.rem(j, 2) == 0
+        return 2 * jnp.where(far_y, 1 - yy, yy) + jnp.where(far_x, xx, 1 - xx)
+
+    own = pl.ds(0, T)
+    other = pl.ds(T, T)
+    l_x = lc(x_h, x2.at[own])
+    l_og = lc(og_h, og2.at[own])
+    l_wkv = lc(wkv_h, wkv_v)
+    l_vec = [
+        lc(src, vecs.at[i]) for i, src in enumerate((g1_h, b1_h, g2_h, b2_h, bq_h, bo_h, bpr_h))
+    ]
+    l_bkv = lc(bkv_h, bkv_v.at[0])
+    l_bfc = lc(bfc_h, bfc_v.at[0])
+    l_mlp = []
+    for j in range(NZ):
+        q = chunk_of(j)
+        cols = pl.ds(pl.multiple_of(Q * (2 * q + c), 128), Q)
+        rows = pl.ds(pl.multiple_of(Q * (2 * q + c), 16), Q)
+        l_mlp.append((lc(wfc_h.at[:, cols], wfc_v.at[q]), lc(wpr_h.at[rows, :], wpr_v.at[q])))
+    l_wq = lc(wq_h, wq_v)
+    l_wo = lc(wo_h, wo_v)
+    l_kvg = lc(kvg_h, kvg_v)
+
+    barrier = pltpu.get_barrier_semaphore()
+    for o in range(1, NSP):
+        pl.semaphore_signal(barrier, inc=1, device_id=sp_peer(o), device_id_type=MESH)
+    for o in range(1, NG):
+        for core in range(2):
+            pl.semaphore_signal(barrier, inc=1, device_id=xy_peer(o, core), device_id_type=MESH)
+    pl.semaphore_wait(barrier, NSP - 1 + 2 * (NG - 1))
+
+    s_x = rc("x", 0, x_h, x2.at[other], partner)
+    send(s_x)
+    s_og = rc("og", 0, og_h, og2.at[other], partner)
+    send(s_og)
+
+    lane = lax.broadcasted_iota(jnp.int32, (8, T), 1)
+    half = lax.broadcasted_iota(jnp.int32, (8, T), 0).astype(F32)
+    block = T // 2
+    first_block = order_s[0, 2 * d]
+    second_block = order_s[0, 2 * d + 1]
+    own_pos = jnp.where(
+        lane < block, first_block * block + lane, second_block * block + (lane - block)
+    )
+    frequency = jnp.exp(half * (-2.0 * rotary_base_log / ROT))
+    angle = own_pos.astype(F32) * 0.25 * frequency
+    cosine, sine = jnp.cos(angle), jnp.sin(angle)
+    cost[...] = cosine
+    sint[...] = sine
+    ones = jnp.ones((HD - ROT, T), F32)
+    zeros = jnp.zeros((HD - ROT, T), F32)
+    ctab[...] = jnp.concatenate([cosine, cosine, ones] * 2, axis=0).T
+    stab[...] = jnp.concatenate([-sine, sine, zeros] * 2, axis=0).T
+    lanes = lax.broadcasted_iota(jnp.int32, (128, pair), 1)
+    low_half = lax.rem(lanes, HD) < ROT // 2
+
+    def turn(tile, rows, sign):
+        mixed = jnp.where(low_half, pltpu.roll(tile, pair - ROT // 2, 1), pltpu.roll(tile, ROT // 2, 1))
+        return tile * ctab[rows, :] + (sign * mixed) * stab[rows, :]
+
+    for copy in l_vec:
+        copy.wait()
+    l_bkv.wait()
+    l_bfc.wait()
+    g1, b1, g2, b2 = (vecs[i : i + 1, :] for i in range(4))
+    vec[...] = jnp.zeros_like(vec)
+
+    def norms(at, keep):
+        for i in range(T // 128):
+            rows = pl.ds(at + 128 * i, 128)
+            v = x2[rows, :].astype(F32)
+            centred = v - jnp.mean(v, axis=-1, keepdims=True)
+            r = lax.rsqrt(jnp.mean(centred * centred, axis=-1, keepdims=True) + norm_eps)
+            n = centred * r
+            first = (n * g1 + b1).astype(BF16)
+            second = (n * g2 + b2).astype(BF16)
+            fi2[rows, :] = first
+            si2[rows, :] = second
+            fit[:, rows] = first.T
+            sit[:, rows] = second.T
+            if keep:
+                nrm[rows, :] = n
+                inv[rows, :] = jnp.broadcast_to(r, (128, 128))
+
+    l_x.wait()
+    norms(0, True)
+
+    l_wkv.wait()
+    for i in range(T // 128):
+        rows = pl.ds(128 * i, 128)
+        kv = mm(fi2[rows, :], wkv_v[...]) + bkv_v[...]
+        kv = jnp.where(lanes < HD, turn(kv, rows, 1.0), kv)
+        kv_all[pl.ds(pl.multiple_of(d * T + 128 * i, 128), 128), :] = kv.astype(BF16)
+    mine = pl.ds(pl.multiple_of(d * T, T), T)
+    s_kv = [rc("kv", o, kv_all.at[mine], kv_all.at[mine], sp_peer(o)) for o in range(1, NSP)]
+    for copy in s_kv:
+        send(copy)
+
+    s_x.wait_recv()
+    norms(T, False)
+    l_og.wait()
+    s_og.wait_recv()
+
+    rows_v, _ = vec_rows(D, F, pair)
+    for pair_of_copies in l_mlp:
+        for copy in pair_of_copies:
+            copy.wait()
+
+    def x_half(q):
+        far = pl.ds(pl.multiple_of(Q // 2 * (1 - xx), 16), Q // 2)
+        return rc("wpx", q, wp_part.at[q, far, :], rx_wp.at[q], xnb)
+
+    def y_chunk(q):
+        side = lax.rem(q, 2)
+        return rc("wfy", side, wf_part.at[q], ry_wf.at[side], ynb)
+
+    def mlp_chunk(j, carry):
+        q = chunk_of(j)
+        at = pl.ds(pl.multiple_of(Q * (2 * q + c), 128), Q)
+        shift = bfc_v[:, at]
+        total = jnp.zeros((1, Q), F32)
+        for i in range(2 * T // 128):
+            rows = pl.ds(128 * i, 128)
+            hidden = mm(si2[rows, :], wfc_v[q]) + shift
+            erf_part = 1.0 + lax.erf(hidden * half_root)
+            act_s[q, rows, :] = (0.5 * hidden * erf_part).astype(BF16)
+            slope = 0.5 * erf_part + hidden * jnp.exp(-0.5 * hidden * hidden) * inv_root_tau
+            act_grad = mm(og2[rows, :], wpr_v[q], NT)
+            hidden_grad = (act_grad * slope).astype(BF16)
+            hg_s[q, rows, :] = hidden_grad
+            total = total + jnp.sum(hidden_grad.astype(F32), axis=0, keepdims=True)
+        for i in range(Q // 128):
+            cols = pl.ds(128 * i, 128)
+            wp_part[q, cols, :] = mm(act_s[q, :, cols], og2[...], TN).astype(BF16)
+        x_half(q).start()
+        for i in range(D // 128):
+            rows = pl.ds(128 * i, 128)
+            wf_part[q, rows, :] = mm(sit[rows, :], hg_s[q]).astype(BF16)
+
+        @pl.when(j < 2)
+        def _():
+            y_chunk(q).start()
+
+        at_row = rows_v["b_fc"][0] + Q // 128 * (2 * q + c)
+        for i in range(Q // 128):
+            vec[pl.ds(at_row + i, 1), :] = total[:, 128 * i : 128 * (i + 1)]
+        return carry
+
+    lax.fori_loop(0, NZ, mlp_chunk, 0)
+
+    def mlp_sums(i, carry):
+        at = lax.rem(i + T // 128, 2 * T // 128) * 128
+        rows = pl.ds(pl.multiple_of(at, 128), 128)
+        out = mm(act_s[0, rows, :], wpr_v[0])
+        back = mm(hg_s[0, rows, :], wfc_v[0], NT)
+        for q in range(1, NZ):
+            out = out + mm(act_s[q, rows, :], wpr_v[q])
+            back = back + mm(hg_s[q, rows, :], wfc_v[q], NT)
+        mlp_all[rows, :] = out
+        sec_all[rows, :] = back
+        return carry
+
+    lax.fori_loop(0, 2 * T // 128, mlp_sums, 0)
+    s_mlp = rc("mlp", 0, mlp_all.at[other], mlp_r, partner)
+    send(s_mlp)
+    s_sec = rc("sec", 0, sec_all.at[other], sec_r, partner)
+    send(s_sec)
+
+    l_wq.wait()
+    l_wo.wait()
+    for i in range(T // 128):
+        rows = pl.ds(128 * i, 128)
+        query = mm(fi2[rows, :], wq_v[...]) + vecs[4:5, :]
+        grads = mm(og2[rows, :], wo_v[...], NT)
+        for t in range(D // pair):
+            q_tile = turn(query[:, pair * t : pair * (t + 1)], rows, 1.0).astype(BF16).astype(F32) * 0.125
+            o_tile = grads[:, pair * t : pair * (t + 1)]
+            low = lanes < HD
+            qo[2 * t, rows, :] = jnp.where(low, q_tile, 0.0).astype(BF16)
+            qo[2 * t + 1, rows, :] = jnp.where(low, pltpu.roll(q_tile, HD, 1), 0.0).astype(BF16)
+            late = pl.ds(T + 128 * i, 128)
+            qo[2 * t, late, :] = jnp.where(low, 0.0, pltpu.roll(o_tile, HD, 1)).astype(BF16)
+            qo[2 * t + 1, late, :] = jnp.where(low, 0.0, o_tile).astype(BF16)
+
+    row_in = lax.broadcasted_iota(jnp.int32, (block, T), 0)
+    query_pos = jnp.broadcast_to(own_pos[0:1, :], (block, T))
+    for j in range(S // block):
+        key_pos = order_s[0, j] * block + row_in
+        bias[pl.ds(block * j, block), :] = jnp.where(key_pos <= query_pos, 0.0, masked_score)
+
+    for copy in s_kv:
+        copy.wait_recv()
+    for j in range(S // 256):
+        rows = pl.ds(256 * j, 256)
+        kvt[:, rows] = kv_all[rows, :].T
+        dkv[rows, :] = jnp.zeros((256, pair), F32)
+
+    near_x = pl.ds(pl.multiple_of(Q // 2 * xx, 16), Q // 2)
+    near_y = pl.ds(pl.multiple_of(Q // 4 * yy, 16), Q // 4)
+    far_y = pl.ds(pl.multiple_of(Q // 4 * (1 - yy), 16), Q // 4)
+
+    def wp_y(q):
+        return rc("wpy", q, wp_s1.at[q, far_y, :], ry_wp.at[q], ynb)
+
+    def wp_first(j):
+        q = chunk_in(j)
+        x_half(q).wait_recv()
+        wp_s1[q] = (wp_part[q, near_x, :].astype(F32) + rx_wp[q].astype(F32)).astype(BF16)
+        wp_y(q).start()
+
+    def wp_z(o):
+        return rc("wpz", o, zs_wp.at[lax.rem(z + o, NZ)], rz_wp.at[o], z_peer(o))
+
+    def wp_second():
+        for q in range(NZ):
+            wp_y(q).wait_recv()
+            zs_wp[q] = (wp_s1[q, near_y, :].astype(F32) + ry_wp[q].astype(F32)).astype(BF16)
+        for o in range(1, NZ):
+            wp_z(o).start()
+
+    slot_wp = 2 * xx + yy
+
+    def wp_g(o):
+        return rc("wpg", o, fin_wp, o_wp.at[slot_wp], xy_peer(o, c))
+
+    l_fin = []
+
+    def wp_third():
+        total = zs_wp[z].astype(F32)
+        for o in range(1, NZ):
+            wp_z(o).wait_recv()
+            total = total + rz_wp[o].astype(F32)
+        fin_wp[...] = total.astype(BF16)
+        for o in range(1, NG):
+            wp_g(o).start()
+        l_fin.append(lc(fin_wp, o_wp.at[slot_wp]))
+
+    wf_x = rc("wfx", 0, wf_s1, rx_wf, xnb)
+
+    def wf_first():
+        q = 2 * yy + 1 - xx
+        y_chunk(2 * (1 - yy) + 1 - xx).wait_recv()
+        wf_s1[...] = (wf_part[q].astype(F32) + ry_wf[1 - xx].astype(F32)).astype(BF16)
+        wf_x.start()
+
+    def wf_second():
+        q = 2 * yy + xx
+        y_chunk(2 * (1 - yy) + xx).wait_recv()
+        wf_own[...] = (wf_part[q].astype(F32) + ry_wf[xx].astype(F32)).astype(BF16)
+
+    def wf_z(o):
+        rows = pl.ds(pl.multiple_of(2 * R * lax.rem(z + o, NZ), 16), 2 * R)
+        return rc("wfz", o, zs_wf.at[rows, :], rz_wf.at[o], z_peer(o))
+
+    def wf_third():
+        wf_x.wait_recv()
+        zs_wf[...] = (wf_own[...].astype(F32) + rx_wf[...].astype(F32)).astype(BF16)
+        for o in range(1, NZ):
+            wf_z(o).start()
+
+    slot_wf = 2 * yy + xx
+
+    def wf_g(o, core):
+        to = c + core - 2 * c * core
+        rows = pl.ds(pl.multiple_of(R * to, 16), R)
+        return rc("wfg", 2 * o + core, fin_wf.at[rows, :], o_wf.at[slot_wf, c], xy_peer(o, to))
+
+    def wf_fourth():
+        total = zs_wf[pl.ds(pl.multiple_of(2 * R * z, 16), 2 * R), :].astype(F32)
+        for o in range(1, NZ):
+            wf_z(o).wait_recv()
+            total = total + rz_wf[o].astype(F32)
+        fin_wf[...] = total.astype(BF16)
+        for o in range(NG):
+            for core in range(2):
+                if o or core:
+                    wf_g(o, core).start()
+        l_fin.append(lc(fin_wf.at[pl.ds(pl.multiple_of(R * c, 16), R), :], o_wf.at[slot_wf, c]))
+
+    def at_head(h):
+        for when, what in EVENTS:
+            pl.when(h == when)(functools.partial(run_event, what))
+
+    def run_event(what):
+        {
+            "wp0": lambda: wp_first(0),
+            "wp1": lambda: wp_first(1),
+            "wp2": lambda: wp_first(2),
+            "wp3": lambda: wp_first(3),
+            "wp_second": wp_second,
+            "wf_first": wf_first,
+            "wf_second": wf_second,
+            "wf_third": wf_third,
+        }[what]()
+
+    KC = 256
+
+    def head(h, carry):
+        at_head(h)
+        both = qo[h]
+        top = jnp.full((8, T), -3e38, F32)
+        for k in range(S // KC):
+            rows = pl.ds(KC * k, KC)
+            sd = mm(kv_all[rows, :], both, NT)
+            score = sd[:, :T] + bias[rows, :]
+            sbuf[rows, :] = score
+            dbuf[rows, :] = sd[:, T:]
+            top = jnp.maximum(top, jnp.max(score.reshape(KC // 8, 8, T), axis=0))
+        top = jnp.max(top, axis=0, keepdims=True)
+        norm = jnp.zeros((8, T), F32)
+        delta = jnp.zeros((8, T), F32)
+        for k in range(S // KC):
+            rows = pl.ds(KC * k, KC)
+            e = jnp.exp(sbuf[rows, :] - top)
+            sbuf[rows, :] = e
+            norm = norm + jnp.sum(e.reshape(KC // 8, 8, T), axis=0)
+            delta = delta + jnp.sum((e * dbuf[rows, :]).reshape(KC // 8, 8, T), axis=0)
+        scale = 1.0 / jnp.sum(norm, axis=0, keepdims=True)
+        delta = jnp.sum(delta, axis=0, keepdims=True) * scale
+        for k in range(S // KC):
+            rows = pl.ds(KC * k, KC)
+            p = sbuf[rows, :] * scale
+            dsp[rows, :T] = (p * (dbuf[rows, :] - delta)).astype(BF16)
+            dsp[rows, T:] = p.astype(BF16)
+        for k in range(S // KC):
+            rows = pl.ds(KC * k, KC)
+            dkv[rows, :] += mm(dsp[rows, :], both)
+        result = mm(kvt[...], dsp[...])
+        rows = pl.ds(pl.multiple_of(HD * h, HD), HD)
+        oht[rows, :] = result[HD:, T:].astype(BF16)
+        back = result[:HD, :T] * 0.125
+        a, b, rest = back[: ROT // 2], back[ROT // 2 : ROT], back[ROT:]
+        ct, st = cost[...], sint[...]
+        qgt[rows, :] = jnp.concatenate([a * ct + b * st, b * ct - a * st, rest], axis=0).astype(BF16)
+        return carry
+
+    lax.fori_loop(0, H, head, 0)
+
+    dkv_b[...] = dkv[...].astype(BF16)
+    s_dkv = []
+    for o in range(1, NSP):
+        rows = pl.ds(pl.multiple_of(lax.rem(d + o, NSP) * T, T), T)
+        s_dkv.append(rc("dkv", o, dkv_b.at[rows, :], rdkv.at[o], sp_peer(o)))
+        send(s_dkv[-1])
+
+    s_ht = []
+    for k in range(NZ):
+        rows = pl.ds(pl.multiple_of(2 * R * k + R * (1 - c), 16), R)
+        s_ht.append(rc("ht", k, oht.at[rows, :], ht_r.at[k], partner))
+        send(s_ht[-1])
+    qg2[own, :] = qgt[...].T
+    s_qg = rc("qg", 0, qg2.at[own], qg2.at[other], partner)
+    send(s_qg)
+
+    wf_fourth()
+    wp_third()
+
+    def put(name, row):
+        at, count = rows_v[name]
+        for i in range(count):
+            vec[at + i : at + i + 1, :] = row[:, 128 * i : 128 * (i + 1)]
+
+    s_mlp.wait_recv()
+    for i in range(T // 128):
+        rows = pl.ds(128 * i, 128)
+        branch = mm(oht[:, rows], wo_v[...], TN) + vecs[5:6, :]
+        mlp = (mlp_all[rows, :] + mlp_r[rows, :]) + vecs[6:7, :]
+        lo_v[rows, :] = ((x2[rows, :].astype(F32) + branch) + mlp).astype(BF16)
+    l_lo = lc(lo_v, o_lo)
+
+    for copy in s_ht:
+        copy.wait_recv()
+    for k in range(NZ):
+        rows = pl.ds(pl.multiple_of(2 * R * k + R * c, 16), R)
+        wo_part[k] = (mm(oht[rows, :], og2[own, :]) + mm(ht_r[k], og2[other, :])).astype(BF16)
+    far_rx = pl.ds(pl.multiple_of(R // 2 * (1 - xx), 16), R // 2)
+    far_ry = pl.ds(pl.multiple_of(R // 2 * (1 - yy), 16), R // 2)
+    near_rx = pl.ds(pl.multiple_of(R // 2 * xx, 16), R // 2)
+    near_ry = pl.ds(pl.multiple_of(R // 2 * yy, 16), R // 2)
+    far_cx = pl.ds(pl.multiple_of(C2 * (1 - xx), 128), C2)
+    far_cy = pl.ds(pl.multiple_of(C2 * (1 - yy), 128), C2)
+    near_cx = pl.ds(pl.multiple_of(C2 * xx, 128), C2)
+    near_cy = pl.ds(pl.multiple_of(C2 * yy, 128), C2)
+    s_wox = rc("wox", 0, wo_part.at[:, far_rx, :], rx_wo, xnb)
+    send(s_wox)
+    s_qg.wait_recv()
+    for k in range(NZ):
+        rows = pl.ds(pl.multiple_of(2 * R * k + R * c, 16), R)
+        wq_part[k] = mm(fit[rows, :], qg2[...]).astype(BF16)
+    s_wqy = rc("wqy", 0, wq_part.at[:, far_ry, :], ry_wq, ynb)
+    send(s_wqy)
+
+    l_kvg.wait()
+    for copy in s_dkv:
+        copy.wait_recv()
+    kv_grads = []
+    for i in range(T // 128):
+        rows = pl.ds(128 * i, 128)
+        total = dkv[pl.ds(pl.multiple_of(d * T + 128 * i, 128), 128), :]
+        for o in range(1, NSP):
+            total = total + rdkv[o, rows, :].astype(F32)
+        total = total + kvg_v[rows, :].astype(F32)
+        kv_grads.append(jnp.where(lanes < HD, turn(total, rows, -1.0), total).astype(BF16))
+    kv_grad = jnp.concatenate(kv_grads, axis=0)
+    put("b_keyval", jnp.sum(kv_grad.astype(F32), axis=0, keepdims=True))
+    wkv_part[...] = mm(fit[:, own], kv_grad)
+    wkv_b[...] = wkv_part[...].astype(BF16)
+    s_wkv = []
+    for o in range(1, NSP):
+        rows = pl.ds(pl.multiple_of(lax.rem(d + o, NSP) * R, 16), R)
+        s_wkv.append(rc("wkv", o, wkv_b.at[rows, :], rkv.at[o], sp_peer(o)))
+        send(s_wkv[-1])
+
+    s_sec.wait_recv()
+    sums = [jnp.zeros((1, D), F32) for _ in range(6)]
+    for i in range(T // 128):
+        rows = pl.ds(128 * i, 128)
+        first_grad = mm(qg2[rows, :], wq_v[...], NT) + mm(kv_grads[i], wkv_v[...], NT)
+        second_grad = sec_all[rows, :] + sec_r[rows, :]
+        n = nrm[rows, :]
+        up = og2[rows, :].astype(F32)
+        u = first_grad * g1 + second_grad * g2
+        back = u - jnp.mean(u, axis=-1, keepdims=True) - n * jnp.mean(u * n, axis=-1, keepdims=True)
+        ig_v[rows, :] = up + inv[rows, 0:1] * back
+        for k, value in enumerate(
+            (first_grad * n, first_grad, qg2[rows, :].astype(F32), up, second_grad * n, second_grad)
+        ):
+            sums[k] = sums[k] + jnp.sum(value, axis=0, keepdims=True)
+    l_ig = lc(ig_v, o_ig)
+    for name, row in zip(("ln1_gain", "ln1_bias", "b_query", "column", "ln2_gain", "ln2_bias"), sums):
+        put(name, row)
+    s_vec = []
+    for o in range(1, NSP):
+        rows = pl.ds(pl.multiple_of(lax.rem(d + o, NSP) * 8, 8), 8)
+        s_vec.append(rc("vec", o, vec.at[rows, :], rvec.at[o], sp_peer(o)))
+        send(s_vec[-1])
+
+    s_wox.wait_recv()
+    wo_s1[...] = (wo_part[:, near_rx, :].astype(F32) + rx_wo[...].astype(F32)).astype(BF16)
+    s_woy = rc("woy", 0, wo_s1.at[:, :, far_cy], ry_wo, ynb)
+    send(s_woy)
+    s_wqy.wait_recv()
+    wq_s1[...] = (wq_part[:, near_ry, :].astype(F32) + ry_wq[...].astype(F32)).astype(BF16)
+    s_wqx = rc("wqx", 0, wq_s1.at[:, :, far_cx], rx_wq, xnb)
+    send(s_wqx)
+
+    for copy in s_wkv:
+        copy.wait_recv()
+    total = wkv_part[pl.ds(pl.multiple_of(d * R, 8), R), :]
+    for o in range(1, NSP):
+        total = total + rkv[o].astype(F32)
+    sm[g, :R, :] = total
+    for copy in s_vec:
+        copy.wait_recv()
+    total = vec[pl.ds(pl.multiple_of(d * 8, 8), 8), :]
+    for o in range(1, NSP):
+        total = total + rvec[o]
+    sm[g, R:, :] = total
+    s_sm = [rc("sm", o, sm.at[g], sm.at[g], xy_peer(o, c)) for o in range(1, NG)]
+    for copy in s_sm:
+        send(copy)
+
+    s_woy.wait_recv()
+    zs_wo[...] = (wo_s1[:, :, near_cy].astype(F32) + ry_wo[...].astype(F32)).astype(BF16)
+    s_woz = []
+    for o in range(1, NZ):
+        s_woz.append(rc("woz", o, zs_wo.at[lax.rem(z + o, NZ)], rz_wo.at[o], z_peer(o)))
+        send(s_woz[-1])
+    s_wqx.wait_recv()
+    zs_wq[...] = (wq_s1[:, :, near_cx].astype(F32) + rx_wq[...].astype(F32)).astype(BF16)
+    s_wqz = []
+    for o in range(1, NZ):
+        s_wqz.append(rc("wqz", o, zs_wq.at[lax.rem(z + o, NZ)], rz_wq.at[o], z_peer(o)))
+        send(s_wqz[-1])
+
+    for copy in s_sm:
+        copy.wait_recv()
+    total = sm[0]
+    for k in range(1, NG):
+        total = total + sm[k]
+    fin_kv[...] = total[:R]
+    fin_vec[...] = total[R:]
+    l_kv = lc(fin_kv, o_wkv)
+    mine8 = pl.ds(pl.multiple_of(d * 8, 8), 8)
+    s_vg = [rc("vg", o, fin_vec, o_vec.at[mine8, :], sp_peer(o)) for o in range(1, NSP)]
+    for copy in s_vg:
+        send(copy)
+    l_vg = lc(fin_vec, o_vec.at[mine8, :])
+
+    total = zs_wo[z].astype(F32)
+    for o in range(1, NZ):
+        s_woz[o - 1].wait_recv()
+        total = total + rz_wo[o].astype(F32)
+    fin_wo[...] = total.astype(BF16)
+    s_wog = [rc("wog", o, fin_wo, o_wo.at[xx, yy], xy_peer(o, c)) for o in range(1, NG)]
+    for copy in s_wog:
+        send(copy)
+    l_fo = lc(fin_wo, o_wo.at[xx, yy])
+    total = zs_wq[z].astype(F32)
+    for o in range(1, NZ):
+        s_wqz[o - 1].wait_recv()
+        total = total + rz_wq[o].astype(F32)
+    fin_wq[...] = total.astype(BF16)
+    s_wqg = [rc("wqg", o, fin_wq, o_wq.at[yy, xx], xy_peer(o, c)) for o in range(1, NG)]
+    for copy in s_wqg:
+        send(copy)
+    l_fq = lc(fin_wq, o_wq.at[yy, xx])
+
+    for o in range(1, NG):
+        wp_g(o).wait_recv()
+    for o in range(NG):
+        for core in range(2):
+            if o or core:
+                wf_g(o, core).wait_recv()
+    for copy in s_wog + s_wqg + s_vg:
+        copy.wait_recv()
+    for copy in started:
+        copy.wait_send()
+    for q in range(NZ):
+        x_half(q).wait_send()
+        wp_y(q).wait_send()
+    for k in range(2):
+        y_chunk(2 * (1 - yy) + k).wait_send()
+    wf_x.wait_send()
+    for o in range(1, NZ):
+        wp_z(o).wait_send()
+        wf_z(o).wait_send()
+    for o in range(1, NG):
+        wp_g(o).wait_send()
+    for o in range(NG):
+        for core in range(2):
+            if o or core:
+                wf_g(o, core).wait_send()
+    for copy in l_fin + [l_lo, l_ig, l_kv, l_vg, l_fo, l_fq]:
+        copy.wait()
+
+
+EVENTS = (
+    (0, "wp0"),
+    (2, "wp1"),
+    (2, "wf_first"),
+    (5, "wp2"),
+    (7, "wp3"),
+    (7, "wf_second"),
+    (9, "wp_second"),
+    (10, "wf_third"),
+)
+
+
+def finish_kernel(
+    dims, wp, wf, wo, wq, wkv, vec, lo, ig,
+    layer_out, input_grad, ln1_gain, ln1_bias, w_query, b_query, w_keyval, b_keyval,
+    w_attn_out, b_attn_out, ln2_gain, ln2_bias, w_fc, b_fc, w_proj, b_proj,
+):
+    T, D, F, S, NSP, NG = dims
+    Q, R, C2 = F // NSP, D // NSP, D // 2
+    layer_out[...] = lo[...]
+    input_grad[...] = ig[...]
+    for k in range(NG):
+        w_proj[Q // NG * k : Q // NG * (k + 1), :] = wp[k].astype(F32)
+        for core in range(2):
+            at = Q * (2 * k + core)
+            w_fc[:, at : at + Q] = wf[k, core].astype(F32)
+    for a in range(2):
+        for b in range(2):
+            rows = slice(R // 2 * a, R // 2 * (a + 1))
+            cols = slice(C2 * b, C2 * (b + 1))
+            w_attn_out[rows, cols] = wo[a, b].astype(F32)
+            w_query[rows, cols] = wq[a, b].astype(F32)
+    w_keyval[...] = wkv[...]
+    rows_v, _ = vec_rows(D, F, 2 * HD)
+    for name, out in (
+        ("ln1_gain", ln1_gain), ("ln1_bias", ln1_bias), ("b_query", b_query), ("b_keyval", b_keyval),
+        ("column", b_attn_out), ("column", b_proj), ("ln2_gain", ln2_gain), ("ln2_bias", ln2_bias),
+        ("b_fc", b_fc),
+    ):
+        at, count = rows_v[name]
+        out[...] = jnp.concatenate([vec[at + i : at + i + 1, :] for i in range(count)], axis=1).reshape(
+            128 * count
+        )
+
+
+def fused_local(n_grp, n_sp, *args):
+    layer_input, block_order = args[0], args[1]
+    T, D = layer_input.shape
+    F = args[12].shape[1]
+    S = T * n_sp
+    NZ, NG, NSP = n_sp // 2, n_grp, n_sp
+    Q, R, C2, pair = F // n_sp, D // n_sp, D // 2, 2 * HD
+    dims = (T, D, F, S, NSP, NG)
+    V = pltpu.VMEM
+    scratch = [
+        V((8, D), F32), V((1, pair), F32), V((1, F), F32),
+        V((2 * T, D), BF16), V((2 * T, D), BF16), V((2 * T, D), BF16), V((2 * T, D), BF16),
+        V((D, 2 * T), BF16), V((D, 2 * T), BF16), V((T, D), F32), V((T, 128), F32),
+        V((D, pair), BF16), V((D, D), BF16), V((D, D), BF16), V((NZ, D, Q), BF16), V((NZ, Q, D), BF16),
+        V((T, pair), BF16), V((NZ, 2 * T, Q), BF16), V((NZ, 2 * T, Q), BF16),
+        V((2 * T, D), F32), V((2 * T, D), F32), V((T, D), F32), V((T, D), F32),
+        V((NZ, Q, D), BF16), V((NZ, Q // 2, D), BF16), V((NZ, Q // 2, D), BF16), V((NZ, Q // 4, D), BF16),
+        V((NZ, Q // 4, D), BF16), V((NZ, Q // 4, D), BF16), V((Q // 4, D), BF16),
+        V((NZ, D, Q), BF16), V((2, D, Q), BF16), V((D, Q), BF16), V((D, Q), BF16), V((D, Q), BF16),
+        V((D, Q), BF16), V((NZ, 2 * R, Q), BF16), V((2 * R, Q), BF16),
+        V((S, pair), BF16), V((pair, S), BF16), V((H, 2 * T, pair), BF16), V((S, T), F32), V((S, T), F32),
+        V((S, T), F32), V((S, 2 * T), BF16), V((S, pair), F32), V((S, pair), BF16), V((NSP, T, pair), BF16),
+        V((D, T), BF16), V((D, T), BF16), V((NZ, R, T), BF16), V((2 * T, D), BF16),
+        V((NZ, R, D), BF16), V((NZ, R // 2, D), BF16), V((NZ, R // 2, D), BF16), V((NZ, R // 2, C2), BF16),
+        V((NZ, R // 2, C2), BF16), V((NZ, R // 2, C2), BF16), V((R // 2, C2), BF16),
+        V((NZ, R, D), BF16), V((NZ, R // 2, D), BF16), V((NZ, R // 2, D), BF16), V((NZ, R // 2, C2), BF16),
+        V((NZ, R // 2, C2), BF16), V((NZ, R // 2, C2), BF16), V((R // 2, C2), BF16),
+        V((8 * NSP, 128), F32), V((NSP, 8, 128), F32), V((D, pair), F32), V((D, pair), BF16),
+        V((NSP, R, pair), BF16), V((NG, R + 8, 128), F32), V((R, 128), F32), V((8, 128), F32),
+        V((T, D), BF16), V((T, D), F32), V((T, pair), F32), V((T, pair), F32), V((8, T), F32), V((8, T), F32),
+        pltpu.SemaphoreType.DMA((40,)), pltpu.SemaphoreType.DMA((128,)), pltpu.SemaphoreType.DMA((128,)),
+    ]
+    any_spec = pl.BlockSpec(memory_space=pl.ANY)
+    shape = jax.ShapeDtypeStruct
+    held = pl.pallas_call(
+        functools.partial(fused_kernel, dims),
+        out_shape=(
+            shape((NG, Q // 4, D), BF16),
+            shape((NG, 2, R, Q), BF16),
+            shape((2, 2, R // 2, C2), BF16),
+            shape((2, 2, R // 2, C2), BF16),
+            shape((R, pair), F32),
+            shape((8 * NSP, 128), F32),
+            shape((T, D), BF16),
+            shape((T, D), F32),
+        ),
+        in_specs=[any_spec, pl.BlockSpec(memory_space=pltpu.SMEM)] + [any_spec] * 16,
+        out_specs=(any_spec,) * 8,
+        scratch_shapes=scratch,
+        compiler_params=pltpu.CompilerParams(
+            collective_id=0, has_side_effects=True, vmem_limit_bytes=67043328
+        ),
+        name="fused_layer",
+    )(*args)
+    vmem_spec = pl.BlockSpec(memory_space=pltpu.VMEM)
+    row = shape((D,), F32)
+    return pl.pallas_call(
+        functools.partial(finish_kernel, dims),
+        out_shape=(
+            shape((T, D), BF16), shape((T, D), F32), row, row, shape((R, D), F32), row, shape((R, pair), F32),
+            shape((pair,), F32), shape((R, D), F32), row, row, row, shape((R, F), F32), shape((F,), F32),
+            shape((Q, D), F32), row,
+        ),
+        in_specs=[vmem_spec] * 8,
+        out_specs=(vmem_spec,) * 16,
+        compiler_params=pltpu.CompilerParams(vmem_limit_bytes=48 << 20),
+        name="finish",
+    )(*held)
+
+
+def fits(mesh, args):
+    n_grp, n_sp = mesh.shape["grp"], mesh.shape["sp"]
+    tokens, width = args[0].shape
+    seqs, blocks = args[1].shape
+    ff = args[12].shape[1]
+    rows = tokens // (n_grp * n_sp)
+    return (
+        n_grp == 4
+        and n_sp == 2 * n_grp
+        and seqs == n_grp
+        and blocks == 2 * n_sp
+        and rows == 2 * 128
+        and width == H * HD
+        and width % (32 * n_sp) == 0
+        and ff % (128 * n_sp) == 0
+        and sum(count for _, count in vec_rows(width, ff, 2 * HD)[0].values()) <= 8 * n_sp
+    )
 
 
 def layer_norm(values, gain_row, shift_row):
@@ -392,27 +1272,37 @@
         P(("grp", "sp"), None),
         P(("grp", "sp"), None),
     )
-    return jax.shard_map(
-        local,
-        mesh=mesh,
-        in_specs=placed,
-        out_specs=(
-            P(("grp", "sp"), None),
-            P(("grp", "sp"), None),
-            P(),
-            P(),
-            P("sp", None),
-            P(),
-            P("sp", None),
-            P(),
-            P("sp", None),
-            P(),
-            P(),
-            P(),
-            P("sp", None),
-            P(),
-            P("sp", None),
-            P(),
-        ),
-        check_vma=False,
-    )
+    def step(*args):
+        if fits(mesh, args):
+            body = functools.partial(fused_local, mesh.shape["grp"], mesh.shape["sp"])
+        else:
+            body = local
+        return spread(body)(*args)
+
+    def spread(body):
+        return jax.shard_map(
+            body,
+            mesh=mesh,
+            in_specs=placed,
+            out_specs=(
+                P(("grp", "sp"), None),
+                P(("grp", "sp"), None),
+                P(),
+                P(),
+                P("sp", None),
+                P(),
+                P("sp", None),
+                P(),
+                P("sp", None),
+                P(),
+                P(),
+                P(),
+                P("sp", None),
+                P(),
+                P("sp", None),
+                P(),
+            ),
+            check_vma=False,
+        )
+
+    return step

time: 595 us -> 132 us (0.22)
  waiting for transfers between devices: 338 us -> 0 us
  Pallas kernels: 0 us -> 123 us
  blocking collectives: 74.6 us -> 0 us
  matrix products: 73 us -> 0 us
  local copies, waits for them, and re-layouts: 47.9 us -> 7.62 us
  other arithmetic: 31.1 us -> 0 us
  between operations: 14.8 us -> 0.84 us
  loops' own time: 11.6 us -> 0 us
    reduce_scatter x6 -> x0, waiting for transfers between devices: 288 us -> none  [the longest x1 101 us: local(): lax.psum_scatter(w_fc_grad, 'sp', scatter_dimension=0, tiled=True)]
    pallas_call x0 -> x2, Pallas kernels: none -> 123 us  [the longest x1 120 us: fused_local(): pl.pallas_call(functools.partial(fused_kernel, dims), out_shape=(shape((N...]
    dot_general x60 -> x0, matrix products: 73 us -> none  [the longest x15 12.5 us: key_scores(): jnp.einsum('rd,kd->rk', query_rows, key_slice[:, :HD], preferred_element_...]
    psum x2 -> x0, blocking collectives: 57.9 us -> none  [the longest x1 39.5 us: local(): lax.psum((jnp.sum(first_grad * first_hat, axis=0), jnp.sum(first_grad, ax...]
    psum x1 -> x0, waiting for transfers between devices: 50.6 us -> none  [local(): lax.psum((query_share, keyval_share, out_share, fc_share, proj_share), 'g...]
    all_gather x1 -> x0, blocking collectives: 16.7 us -> none  [local(): lax.all_gather(keyval_use.reshape(seq_count, shard_len, pair_width), 'sp'...]
    another operation x10 -> x0, loops' own time: 11.6 us -> none  [the longest x1 5.35 us: attention_forward(): lax.map(one_pair, (query_tiles, tile_pos, jnp.arange(pair_count, dtype=jn...]
    dynamic_update_slice x7 -> x0, other arithmetic: 8.55 us -> none  [the longest x5 8.5 us: grad_pass(): lax.dynamic_update_slice(sequence_grads, updated, (sequence, key_start, 0))]
  transfers between devices with their start and end apart: 7 -> 0, of which waited for: 6 -> 0; matrix products, arithmetic and copies ran while one was open for 9% -> 0% of each run, Pallas kernels for 0% -> 0%
where the time goes in v1:
time: 132 us; the launch traced here: 131 us
  Pallas kernels  123 us (93%)
  local copies, waits for them, and re-layouts  7.62 us (6%)
    pallas_call x1, Pallas kernels, fused_local(): pl.pallas_call(functools.partial(fused_kernel, dims), out_shape=(shape((N...  120 us
    unnamed x16, local copies, waits for them, and re-layouts  7.62 us

profile of v1, /device:TPU:0, one launch (start us, length us, event | category | flops | bytes accessed | tf_op | source)
XLA Modules:
  0.0 131.1 jit_solution(14884589857206315021)
XLA Ops:
  0.7 120.5 %fused_layer.1 = (bf16[4,96,768]{2,1,0:T(8,128)(2,1)}, bf16[4,2,96,384]{3,2,1,0:T(8,128)(2,1)}, bf16[2,2,48,384]{3,2,1,0:T(8,128)(2,1)}, bf16[2,2,48,384]{3,2,1,...) custom-call(bf16[256,768]{1,0:T(8,128)(2,1)} %x_h.1, ...), custom_call_target="tpu_custom_call" | custom-call | tf_op jit(solution)/shard_map/fused_layer/pallas_call | solution.py:846
  121.1 0.0 copy-start
  121.1 1.1 copy-done
  122.3 0.0 copy-start.1
  122.3 1.1 copy-done.1
  123.3 0.0 copy-start.2
  123.3 1.1 copy-done.2
  124.4 0.0 copy-start.3
  124.4 1.0 copy-done.3
  125.4 0.0 copy-start.4
  125.4 0.9 copy-done.4
  126.3 0.0 copy-start.5
  126.3 0.9 copy-done.5
  127.2 0.0 copy-start.6
  127.2 0.8 copy-done.6
  128.0 0.0 copy-start.7
  128.0 0.8 copy-done.7
  128.8 2.2 %finish.1 = (bf16[256,768]{1,0:T(8,128)(2,1)}, f32[256,768]{1,0:T(8,128)}, f32[768]{0:T(1024)}, f32[768]{0:T(1024)}, f32[96,768]{1,0:T(8,128)}, /*index=5*/f32[7...) custom-call(bf16[4,96,768]{2,1,0:T(8,128)(2,1)S(1)} %copy-done.1, ...), custom_call_target="tpu_custom_call" | custom-call | tf_op jit(solution)/shard_map/finish/pallas_call | solution.py:868
Async XLA Ops:
  121.1 1.1 copy-start
  122.3 1.1 copy-start.1
  123.3 1.1 copy-start.2
  124.4 1.0 copy-start.3
  125.4 0.9 copy-start.4
  126.3 0.9 copy-start.5
  127.2 0.8 copy-start.6
  128.0 0.8 copy-start.7

commit v2 on v1

--- a/solution.py
+++ b/solution.py
@@ -97,12 +97,18 @@
     ry_wp,
     zs_wp,
     rz_wp,
+    rzf,
+    zf_s0,
+    rx_zf,
+    zf_s1,
+    ry_zf,
     fin_wp,
     wf_part,
     ry_wf,
+    rx_wf,
     wf_s1,
     wf_own,
-    rx_wf,
+    wf_in,
     zs_wf,
     rz_wf,
     fin_wf,
@@ -115,7 +121,10 @@
     dsp,
     dkv,
     dkv_b,
+    rdk,
+    dks,
     rdkv,
+    kvg2,
     oht,
     qgt,
     ht_r,
@@ -154,7 +163,9 @@
 ):
     T, D, F, S, NSP, NG = dims
     NZ = NSP // 2
+    D2 = D // 2
     Q = F // NSP
+    QH = Q // 2
     R = D // NSP
     C2 = D // 2
     pair = 2 * HD
@@ -187,11 +198,12 @@
     for name, n in (
         ("x", 1), ("og", 1), ("kv", NSP), ("mlp", 1), ("sec", 1),
         ("wpx", NZ), ("wpy", NZ), ("wpz", NZ), ("wpg", NG),
-        ("wfy", 2), ("wfx", 1), ("wfz", NZ), ("wfg", 2 * NG),
-        ("ht", NZ), ("qg", 1), ("dkv", NSP),
+        ("wpf", NZ), ("zfx", 1), ("zfy", 1),
+        ("wfy", 2), ("wfx", 2), ("wfs", 2), ("wfz", NZ), ("wfg", 2 * NG),
+        ("ht", NZ), ("qg", 1), ("dk", NZ), ("dkv", NZ), ("kvg", 1),
         ("wox", 1), ("woy", 1), ("woz", NZ), ("wog", NG),
         ("wqy", 1), ("wqx", 1), ("wqz", NZ), ("wqg", NG),
-        ("wkv", NSP), ("vec", NSP), ("sm", NG), ("vg", NSP),
+        ("wkv", NZ), ("vec", NSP), ("sm", NG), ("vg", NSP),
     ):
         take(name, n)
 
@@ -336,12 +348,23 @@
             copy.wait()
 
     def x_half(q):
-        far = pl.ds(pl.multiple_of(Q // 2 * (1 - xx), 16), Q // 2)
+        far = pl.ds(pl.multiple_of(QH // 2 * (1 - xx), 16), QH // 2)
         return rc("wpx", q, wp_part.at[q, far, :], rx_wp.at[q], xnb)
+
+    def z_half(o):
+        q = lax.rem(z + o, NZ)
+        return rc("wpf", o, wp_part.at[q, pl.ds(QH, QH), :], rzf.at[o], z_peer(o))
 
     def y_chunk(q):
         side = lax.rem(q, 2)
-        return rc("wfy", side, wf_part.at[q], ry_wf.at[side], ynb)
+        return rc("wfy", side, wf_part.at[q, pl.ds(0, D2), :], ry_wf.at[side], ynb)
+
+    def x_chunk(q):
+        side = lax.div(q, 2)
+        return rc("wfx", side, wf_part.at[q, pl.ds(D2, D2), :], rx_wf.at[side], xnb)
+
+    def start_z_half(o):
+        z_half(o).start()
 
     def mlp_chunk(j, carry):
         q = chunk_of(j)
@@ -362,6 +385,8 @@
             cols = pl.ds(128 * i, 128)
             wp_part[q, cols, :] = mm(act_s[q, :, cols], og2[...], TN).astype(BF16)
         x_half(q).start()
+        for o in range(1, NZ):
+            pl.when(lax.rem(z + o, NZ) == q)(functools.partial(start_z_half, o))
         for i in range(D // 128):
             rows = pl.ds(128 * i, 128)
             wf_part[q, rows, :] = mm(sit[rows, :], hg_s[q]).astype(BF16)
@@ -369,6 +394,10 @@
         @pl.when(j < 2)
         def _():
             y_chunk(q).start()
+
+        @pl.when(lax.rem(j, 2) == 0)
+        def _():
+            x_chunk(q).start()
 
         at_row = rows_v["b_fc"][0] + Q // 128 * (2 * q + c)
         for i in range(Q // 128):
@@ -424,9 +453,9 @@
         kvt[:, rows] = kv_all[rows, :].T
         dkv[rows, :] = jnp.zeros((256, pair), F32)
 
-    near_x = pl.ds(pl.multiple_of(Q // 2 * xx, 16), Q // 2)
-    near_y = pl.ds(pl.multiple_of(Q // 4 * yy, 16), Q // 4)
-    far_y = pl.ds(pl.multiple_of(Q // 4 * (1 - yy), 16), Q // 4)
+    near_x = pl.ds(pl.multiple_of(QH // 2 * xx, 16), QH // 2)
+    near_y = pl.ds(pl.multiple_of(QH // 4 * yy, 16), QH // 4)
+    far_y = pl.ds(pl.multiple_of(QH // 4 * (1 - yy), 16), QH // 4)
 
     def wp_y(q):
         return rc("wpy", q, wp_s1.at[q, far_y, :], ry_wp.at[q], ynb)
@@ -454,38 +483,76 @@
 
     l_fin = []
 
+    far_zx = pl.ds(pl.multiple_of(QH // 2 * (1 - xx), 16), QH // 2)
+    zf_x = rc("zfx", 0, zf_s0.at[far_zx, :], rx_zf, xnb)
+    zf_y = rc("zfy", 0, zf_s1.at[far_y, :], ry_zf, ynb)
+
+    def zf_first():
+        total = wp_part[z, QH:, :].astype(F32)
+        for o in range(1, NZ):
+            z_half(o).wait_recv()
+            total = total + rzf[o].astype(F32)
+        zf_s0[...] = total.astype(BF16)
+        zf_x.start()
+
+    def zf_second():
+        zf_x.wait_recv()
+        zf_s1[...] = (zf_s0[near_x, :].astype(F32) + rx_zf[...].astype(F32)).astype(BF16)
+        zf_y.start()
+
+    def zf_third():
+        zf_y.wait_recv()
+        fin_wp[1] = (zf_s1[near_y, :].astype(F32) + ry_zf[...].astype(F32)).astype(BF16)
+
     def wp_third():
         total = zs_wp[z].astype(F32)
         for o in range(1, NZ):
             wp_z(o).wait_recv()
             total = total + rz_wp[o].astype(F32)
-        fin_wp[...] = total.astype(BF16)
+        fin_wp[0] = total.astype(BF16)
         for o in range(1, NG):
             wp_g(o).start()
         l_fin.append(lc(fin_wp, o_wp.at[slot_wp]))
 
-    wf_x = rc("wfx", 0, wf_s1, rx_wf, xnb)
-
-    def wf_first():
-        q = 2 * yy + 1 - xx
-        y_chunk(2 * (1 - yy) + 1 - xx).wait_recv()
-        wf_s1[...] = (wf_part[q].astype(F32) + ry_wf[1 - xx].astype(F32)).astype(BF16)
-        wf_x.start()
-
-    def wf_second():
+    def wf_second_send(part):
+        return rc("wfs", part, wf_s1.at[part], wf_in.at[part], ynb if part else xnb)
+
+    def wf_first(part):
+        if part:
+            q = 2 * (1 - yy) + xx
+            x_chunk(2 * (1 - yy) + 1 - xx).wait_recv()
+            got = rx_wf[1 - yy]
+        else:
+            q = 2 * yy + 1 - xx
+            y_chunk(2 * (1 - yy) + 1 - xx).wait_recv()
+            got = ry_wf[1 - xx]
+        wf_s1[part] = (wf_part[q, D2 * part : D2 * (part + 1), :].astype(F32) + got.astype(F32)).astype(BF16)
+        wf_second_send(part).start()
+
+    def wf_second(part):
         q = 2 * yy + xx
-        y_chunk(2 * (1 - yy) + xx).wait_recv()
-        wf_own[...] = (wf_part[q].astype(F32) + ry_wf[xx].astype(F32)).astype(BF16)
+        if part:
+            x_chunk(2 * yy + 1 - xx).wait_recv()
+            got = rx_wf[yy]
+        else:
+            y_chunk(2 * (1 - yy) + xx).wait_recv()
+            got = ry_wf[xx]
+        wf_own[part] = (wf_part[q, D2 * part : D2 * (part + 1), :].astype(F32) + got.astype(F32)).astype(BF16)
 
     def wf_z(o):
         rows = pl.ds(pl.multiple_of(2 * R * lax.rem(z + o, NZ), 16), 2 * R)
         return rc("wfz", o, zs_wf.at[rows, :], rz_wf.at[o], z_peer(o))
 
-    def wf_third():
-        wf_x.wait_recv()
-        zs_wf[...] = (wf_own[...].astype(F32) + rx_wf[...].astype(F32)).astype(BF16)
+    def start_wf_z(o):
+        wf_z(o).start()
+
+    def wf_third(part):
+        wf_second_send(part).wait_recv()
+        zs_wf[D2 * part : D2 * (part + 1), :] = (
+            wf_own[part].astype(F32) + wf_in[part].astype(F32)
+        ).astype(BF16)
         for o in range(1, NZ):
-            wf_z(o).start()
+            pl.when(lax.div(lax.rem(z + o, NZ), NZ // 2) == part)(functools.partial(start_wf_z, o))
 
     slot_wf = 2 * yy + xx
 
@@ -517,9 +584,15 @@
             "wp2": lambda: wp_first(2),
             "wp3": lambda: wp_first(3),
             "wp_second": wp_second,
-            "wf_first": wf_first,
-            "wf_second": wf_second,
-            "wf_third": wf_third,
+            "zf_first": zf_first,
+            "zf_second": zf_second,
+            "zf_third": zf_third,
+            "wf_first0": lambda: wf_first(0),
+            "wf_second0": lambda: wf_second(0),
+            "wf_third0": lambda: wf_third(0),
+            "wf_first1": lambda: wf_first(1),
+            "wf_second1": lambda: wf_second(1),
+            "wf_third1": lambda: wf_third(1),
         }[what]()
 
     KC = 256
@@ -565,12 +638,14 @@
 
     lax.fori_loop(0, H, head, 0)
 
+    def block_rows(k, core):
+        return pl.ds(pl.multiple_of((2 * k + core) * T, T), T)
+
     dkv_b[...] = dkv[...].astype(BF16)
-    s_dkv = []
-    for o in range(1, NSP):
-        rows = pl.ds(pl.multiple_of(lax.rem(d + o, NSP) * T, T), T)
-        s_dkv.append(rc("dkv", o, dkv_b.at[rows, :], rdkv.at[o], sp_peer(o)))
-        send(s_dkv[-1])
+    s_dk = []
+    for k in range(NZ):
+        s_dk.append(rc("dk", k, dkv_b.at[block_rows(k, 1 - c), :], rdk.at[k], partner))
+        send(s_dk[-1])
 
     s_ht = []
     for k in range(NZ):
@@ -581,21 +656,19 @@
     s_qg = rc("qg", 0, qg2.at[own], qg2.at[other], partner)
     send(s_qg)
 
-    wf_fourth()
-    wp_third()
+    for copy in s_dk:
+        copy.wait_recv()
+    s_dkv = []
+    for o in range(1, NZ):
+        k = lax.rem(z + o, NZ)
+        dks[o] = (dkv[block_rows(k, c), :] + rdk[k].astype(F32)).astype(BF16)
+        s_dkv.append(rc("dkv", o, dks.at[o], rdkv.at[o], z_peer(o)))
+        send(s_dkv[-1])
 
     def put(name, row):
         at, count = rows_v[name]
         for i in range(count):
             vec[at + i : at + i + 1, :] = row[:, 128 * i : 128 * (i + 1)]
-
-    s_mlp.wait_recv()
-    for i in range(T // 128):
-        rows = pl.ds(128 * i, 128)
-        branch = mm(oht[:, rows], wo_v[...], TN) + vecs[5:6, :]
-        mlp = (mlp_all[rows, :] + mlp_r[rows, :]) + vecs[6:7, :]
-        lo_v[rows, :] = ((x2[rows, :].astype(F32) + branch) + mlp).astype(BF16)
-    l_lo = lc(lo_v, o_lo)
 
     for copy in s_ht:
         copy.wait_recv()
@@ -619,26 +692,56 @@
     s_wqy = rc("wqy", 0, wq_part.at[:, far_ry, :], ry_wq, ynb)
     send(s_wqy)
 
+    zf_third()
+
+    s_mlp.wait_recv()
+    for i in range(T // 128):
+        rows = pl.ds(128 * i, 128)
+        branch = mm(oht[:, rows], wo_v[...], TN) + vecs[5:6, :]
+        mlp = (mlp_all[rows, :] + mlp_r[rows, :]) + vecs[6:7, :]
+        lo_v[rows, :] = ((x2[rows, :].astype(F32) + branch) + mlp).astype(BF16)
+    l_lo = lc(lo_v, o_lo)
+
+    s_wox.wait_recv()
+    wo_s1[...] = (wo_part[:, near_rx, :].astype(F32) + rx_wo[...].astype(F32)).astype(BF16)
+    s_woy = rc("woy", 0, wo_s1.at[:, :, far_cy], ry_wo, ynb)
+    send(s_woy)
+    s_wqy.wait_recv()
+    wq_s1[...] = (wq_part[:, near_ry, :].astype(F32) + ry_wq[...].astype(F32)).astype(BF16)
+    s_wqx = rc("wqx", 0, wq_s1.at[:, :, far_cx], rx_wq, xnb)
+    send(s_wqx)
+
+    s_woy.wait_recv()
+    zs_wo[...] = (wo_s1[:, :, near_cy].astype(F32) + ry_wo[...].astype(F32)).astype(BF16)
+    s_woz = []
+    for o in range(1, NZ):
+        s_woz.append(rc("woz", o, zs_wo.at[lax.rem(z + o, NZ)], rz_wo.at[o], z_peer(o)))
+        send(s_woz[-1])
+    s_wqx.wait_recv()
+    zs_wq[...] = (wq_s1[:, :, near_cx].astype(F32) + rx_wq[...].astype(F32)).astype(BF16)
+    s_wqz = []
+    for o in range(1, NZ):
+        s_wqz.append(rc("wqz", o, zs_wq.at[lax.rem(z + o, NZ)], rz_wq.at[o], z_peer(o)))
+        send(s_wqz[-1])
+
+    wp_third()
+    wf_fourth()
+
     l_kvg.wait()
     for copy in s_dkv:
         copy.wait_recv()
     kv_grads = []
     for i in range(T // 128):
         rows = pl.ds(128 * i, 128)
-        total = dkv[pl.ds(pl.multiple_of(d * T + 128 * i, 128), 128), :]
-        for o in range(1, NSP):
+        total = dkv[pl.ds(pl.multiple_of(d * T + 128 * i, 128), 128), :] + rdk[z, rows, :].astype(F32)
+        for o in range(1, NZ):
             total = total + rdkv[o, rows, :].astype(F32)
         total = total + kvg_v[rows, :].astype(F32)
         kv_grads.append(jnp.where(lanes < HD, turn(total, rows, -1.0), total).astype(BF16))
-    kv_grad = jnp.concatenate(kv_grads, axis=0)
-    put("b_keyval", jnp.sum(kv_grad.astype(F32), axis=0, keepdims=True))
-    wkv_part[...] = mm(fit[:, own], kv_grad)
-    wkv_b[...] = wkv_part[...].astype(BF16)
-    s_wkv = []
-    for o in range(1, NSP):
-        rows = pl.ds(pl.multiple_of(lax.rem(d + o, NSP) * R, 16), R)
-        s_wkv.append(rc("wkv", o, wkv_b.at[rows, :], rkv.at[o], sp_peer(o)))
-        send(s_wkv[-1])
+        kvg2[rows, :] = kv_grads[-1]
+    s_kvg = rc("kvg", 0, kvg2.at[own], kvg2.at[other], partner)
+    send(s_kvg)
+    put("b_keyval", jnp.sum(jnp.concatenate(kv_grads, axis=0).astype(F32), axis=0, keepdims=True))
 
     s_sec.wait_recv()
     sums = [jnp.zeros((1, D), F32) for _ in range(6)]
@@ -664,19 +767,20 @@
         s_vec.append(rc("vec", o, vec.at[rows, :], rvec.at[o], sp_peer(o)))
         send(s_vec[-1])
 
-    s_wox.wait_recv()
-    wo_s1[...] = (wo_part[:, near_rx, :].astype(F32) + rx_wo[...].astype(F32)).astype(BF16)
-    s_woy = rc("woy", 0, wo_s1.at[:, :, far_cy], ry_wo, ynb)
-    send(s_woy)
-    s_wqy.wait_recv()
-    wq_s1[...] = (wq_part[:, near_ry, :].astype(F32) + ry_wq[...].astype(F32)).astype(BF16)
-    s_wqx = rc("wqx", 0, wq_s1.at[:, :, far_cx], rx_wq, xnb)
-    send(s_wqx)
+    s_kvg.wait_recv()
+    s_wkv = []
+    for k in range(NZ):
+        rows = pl.ds(pl.multiple_of(2 * R * k + R * c, 16), R)
+        wkv_part[k] = mm(fit[rows, :], kvg2[...])
+        wkv_b[k] = wkv_part[k].astype(BF16)
+    for o in range(1, NZ):
+        s_wkv.append(rc("wkv", o, wkv_b.at[lax.rem(z + o, NZ)], rkv.at[o], z_peer(o)))
+        send(s_wkv[-1])
 
     for copy in s_wkv:
         copy.wait_recv()
-    total = wkv_part[pl.ds(pl.multiple_of(d * R, 8), R), :]
-    for o in range(1, NSP):
+    total = wkv_part[z]
+    for o in range(1, NZ):
         total = total + rkv[o].astype(F32)
     sm[g, :R, :] = total
     for copy in s_vec:
@@ -688,33 +792,6 @@
     s_sm = [rc("sm", o, sm.at[g], sm.at[g], xy_peer(o, c)) for o in range(1, NG)]
     for copy in s_sm:
         send(copy)
-
-    s_woy.wait_recv()
-    zs_wo[...] = (wo_s1[:, :, near_cy].astype(F32) + ry_wo[...].astype(F32)).astype(BF16)
-    s_woz = []
-    for o in range(1, NZ):
-        s_woz.append(rc("woz", o, zs_wo.at[lax.rem(z + o, NZ)], rz_wo.at[o], z_peer(o)))
-        send(s_woz[-1])
-    s_wqx.wait_recv()
-    zs_wq[...] = (wq_s1[:, :, near_cx].astype(F32) + rx_wq[...].astype(F32)).astype(BF16)
-    s_wqz = []
-    for o in range(1, NZ):
-        s_wqz.append(rc("wqz", o, zs_wq.at[lax.rem(z + o, NZ)], rz_wq.at[o], z_peer(o)))
-        send(s_wqz[-1])
-
-    for copy in s_sm:
-        copy.wait_recv()
-    total = sm[0]
-    for k in range(1, NG):
-        total = total + sm[k]
-    fin_kv[...] = total[:R]
-    fin_vec[...] = total[R:]
-    l_kv = lc(fin_kv, o_wkv)
-    mine8 = pl.ds(pl.multiple_of(d * 8, 8), 8)
-    s_vg = [rc("vg", o, fin_vec, o_vec.at[mine8, :], sp_peer(o)) for o in range(1, NSP)]
-    for copy in s_vg:
-        send(copy)
-    l_vg = lc(fin_vec, o_vec.at[mine8, :])
 
     total = zs_wo[z].astype(F32)
     for o in range(1, NZ):
@@ -735,6 +812,20 @@
         send(copy)
     l_fq = lc(fin_wq, o_wq.at[yy, xx])
 
+    for copy in s_sm:
+        copy.wait_recv()
+    total = sm[0]
+    for k in range(1, NG):
+        total = total + sm[k]
+    fin_kv[...] = total[:R]
+    fin_vec[...] = total[R:]
+    l_kv = lc(fin_kv, o_wkv)
+    mine8 = pl.ds(pl.multiple_of(d * 8, 8), 8)
+    s_vg = [rc("vg", o, fin_vec, o_vec.at[mine8, :], sp_peer(o)) for o in range(1, NSP)]
+    for copy in s_vg:
+        send(copy)
+    l_vg = lc(fin_vec, o_vec.at[mine8, :])
+
     for o in range(1, NG):
         wp_g(o).wait_recv()
     for o in range(NG):
@@ -750,8 +841,12 @@
         wp_y(q).wait_send()
     for k in range(2):
         y_chunk(2 * (1 - yy) + k).wait_send()
-    wf_x.wait_send()
+        x_chunk(2 * k + 1 - xx).wait_send()
+        wf_second_send(k).wait_send()
+    zf_x.wait_send()
+    zf_y.wait_send()
     for o in range(1, NZ):
+        z_half(o).wait_send()
         wp_z(o).wait_send()
         wf_z(o).wait_send()
     for o in range(1, NG):
@@ -766,37 +861,72 @@
 
 EVENTS = (
     (0, "wp0"),
-    (2, "wp1"),
-    (2, "wf_first"),
-    (5, "wp2"),
-    (7, "wp3"),
-    (7, "wf_second"),
-    (9, "wp_second"),
-    (10, "wf_third"),
+    (1, "wf_first0"),
+    (1, "wf_first1"),
+    (1, "wp1"),
+    (2, "wf_second0"),
+    (3, "wp2"),
+    (5, "wf_second1"),
+    (5, "wp3"),
+    (6, "wf_third1"),
+    (7, "wp_second"),
+    (8, "wf_third0"),
+    (9, "zf_first"),
+    (11, "zf_second"),
 )
 
 
 def finish_kernel(
-    dims, wp, wf, wo, wq, wkv, vec, lo, ig,
+    dims, wp_h, wf_h, wo_h, wq_h, wkv_h, vec_h, lo_h, ig_h,
     layer_out, input_grad, ln1_gain, ln1_bias, w_query, b_query, w_keyval, b_keyval,
     w_attn_out, b_attn_out, ln2_gain, ln2_bias, w_fc, b_fc, w_proj, b_proj,
+    wp, wf, wo, wq, wkv, vec, lo, ig, fc_v, proj_v, out_v, query_v, isem, osem,
 ):
     T, D, F, S, NSP, NG = dims
     Q, R, C2 = F // NSP, D // NSP, D // 2
-    layer_out[...] = lo[...]
-    input_grad[...] = ig[...]
+    arrive = {}
+    for i, (name, src, dst) in enumerate(
+        (("wf", wf_h, wf), ("wp", wp_h, wp), ("ig", ig_h, ig), ("lo", lo_h, lo), ("vec", vec_h, vec),
+         ("wo", wo_h, wo), ("wq", wq_h, wq), ("wkv", wkv_h, wkv))
+    ):
+        arrive[name] = pltpu.make_async_copy(src, dst, isem.at[i])
+        arrive[name].start()
+    leave = []
+
+    def put_out(src, dst):
+        leave.append(pltpu.make_async_copy(src, dst, osem.at[len(leave)]))
+        leave[-1].start()
+
+    arrive["wf"].wait()
     for k in range(NG):
-        w_proj[Q // NG * k : Q // NG * (k + 1), :] = wp[k].astype(F32)
         for core in range(2):
             at = Q * (2 * k + core)
-            w_fc[:, at : at + Q] = wf[k, core].astype(F32)
+            fc_v[:, at : at + Q] = wf[k, core].astype(F32)
+    put_out(fc_v, w_fc)
+    arrive["wp"].wait()
+    rows = Q // 2 // NG
+    for k in range(NG):
+        for part in range(2):
+            at = Q // 2 * part + rows * k
+            proj_v[at : at + rows, :] = wp[k, part].astype(F32)
+    put_out(proj_v, w_proj)
+    arrive["ig"].wait()
+    put_out(ig, input_grad)
+    arrive["lo"].wait()
+    put_out(lo, layer_out)
+    arrive["wo"].wait()
+    arrive["wq"].wait()
     for a in range(2):
         for b in range(2):
             rows = slice(R // 2 * a, R // 2 * (a + 1))
             cols = slice(C2 * b, C2 * (b + 1))
-            w_attn_out[rows, cols] = wo[a, b].astype(F32)
-            w_query[rows, cols] = wq[a, b].astype(F32)
-    w_keyval[...] = wkv[...]
+            out_v[rows, cols] = wo[a, b].astype(F32)
+            query_v[rows, cols] = wq[a, b].astype(F32)
+    put_out(out_v, w_attn_out)
+    put_out(query_v, w_query)
+    arrive["wkv"].wait()
+    put_out(wkv, w_keyval)
+    arrive["vec"].wait()
     rows_v, _ = vec_rows(D, F, 2 * HD)
     for name, out in (
         ("ln1_gain", ln1_gain), ("ln1_bias", ln1_bias), ("b_query", b_query), ("b_keyval", b_keyval),
@@ -807,6 +937,8 @@
         out[...] = jnp.concatenate([vec[at + i : at + i + 1, :] for i in range(count)], axis=1).reshape(
             128 * count
         )
+    for copy in leave:
+        copy.wait()
 
 
 def fused_local(n_grp, n_sp, *args):
@@ -825,19 +957,21 @@
         V((D, pair), BF16), V((D, D), BF16), V((D, D), BF16), V((NZ, D, Q), BF16), V((NZ, Q, D), BF16),
         V((T, pair), BF16), V((NZ, 2 * T, Q), BF16), V((NZ, 2 * T, Q), BF16),
         V((2 * T, D), F32), V((2 * T, D), F32), V((T, D), F32), V((T, D), F32),
-        V((NZ, Q, D), BF16), V((NZ, Q // 2, D), BF16), V((NZ, Q // 2, D), BF16), V((NZ, Q // 4, D), BF16),
-        V((NZ, Q // 4, D), BF16), V((NZ, Q // 4, D), BF16), V((Q // 4, D), BF16),
-        V((NZ, D, Q), BF16), V((2, D, Q), BF16), V((D, Q), BF16), V((D, Q), BF16), V((D, Q), BF16),
-        V((D, Q), BF16), V((NZ, 2 * R, Q), BF16), V((2 * R, Q), BF16),
+        V((NZ, Q, D), BF16), V((NZ, Q // 4, D), BF16), V((NZ, Q // 4, D), BF16), V((NZ, Q // 8, D), BF16),
+        V((NZ, Q // 8, D), BF16), V((NZ, Q // 8, D), BF16), V((NZ, Q // 2, D), BF16), V((Q // 2, D), BF16),
+        V((Q // 4, D), BF16), V((Q // 4, D), BF16), V((Q // 8, D), BF16), V((2, Q // 8, D), BF16),
+        V((NZ, D, Q), BF16), V((2, D // 2, Q), BF16), V((2, D // 2, Q), BF16), V((2, D // 2, Q), BF16),
+        V((2, D // 2, Q), BF16), V((2, D // 2, Q), BF16), V((D, Q), BF16), V((NZ, 2 * R, Q), BF16), V((2 * R, Q), BF16),
         V((S, pair), BF16), V((pair, S), BF16), V((H, 2 * T, pair), BF16), V((S, T), F32), V((S, T), F32),
-        V((S, T), F32), V((S, 2 * T), BF16), V((S, pair), F32), V((S, pair), BF16), V((NSP, T, pair), BF16),
+        V((S, T), F32), V((S, 2 * T), BF16), V((S, pair), F32), V((S, pair), BF16), V((NZ, T, pair), BF16),
+        V((NZ, T, pair), BF16), V((NZ, T, pair), BF16), V((2 * T, pair), BF16),
         V((D, T), BF16), V((D, T), BF16), V((NZ, R, T), BF16), V((2 * T, D), BF16),
         V((NZ, R, D), BF16), V((NZ, R // 2, D), BF16), V((NZ, R // 2, D), BF16), V((NZ, R // 2, C2), BF16),
         V((NZ, R // 2, C2), BF16), V((NZ, R // 2, C2), BF16), V((R // 2, C2), BF16),
         V((NZ, R, D), BF16), V((NZ, R // 2, D), BF16), V((NZ, R // 2, D), BF16), V((NZ, R // 2, C2), BF16),
         V((NZ, R // 2, C2), BF16), V((NZ, R // 2, C2), BF16), V((R // 2, C2), BF16),
-        V((8 * NSP, 128), F32), V((NSP, 8, 128), F32), V((D, pair), F32), V((D, pair), BF16),
-        V((NSP, R, pair), BF16), V((NG, R + 8, 128), F32), V((R, 128), F32), V((8, 128), F32),
+        V((8 * NSP, 128), F32), V((NSP, 8, 128), F32), V((NZ, R, pair), F32), V((NZ, R, pair), BF16),
+        V((NZ, R, pair), BF16), V((NG, R + 8, 128), F32), V((R, 128), F32), V((8, 128), F32),
         V((T, D), BF16), V((T, D), F32), V((T, pair), F32), V((T, pair), F32), V((8, T), F32), V((8, T), F32),
         pltpu.SemaphoreType.DMA((40,)), pltpu.SemaphoreType.DMA((128,)), pltpu.SemaphoreType.DMA((128,)),
     ]
@@ -846,7 +980,7 @@
     held = pl.pallas_call(
         functools.partial(fused_kernel, dims),
         out_shape=(
-            shape((NG, Q // 4, D), BF16),
+            shape((NG, 2, Q // 8, D), BF16),
             shape((NG, 2, R, Q), BF16),
             shape((2, 2, R // 2, C2), BF16),
             shape((2, 2, R // 2, C2), BF16),
@@ -872,9 +1006,15 @@
             shape((pair,), F32), shape((R, D), F32), row, row, row, shape((R, F), F32), shape((F,), F32),
             shape((Q, D), F32), row,
         ),
-        in_specs=[vmem_spec] * 8,
-        out_specs=(vmem_spec,) * 16,
-        compiler_params=pltpu.CompilerParams(vmem_limit_bytes=48 << 20),
+        in_specs=[any_spec] * 8,
+        out_specs=tuple(any_spec if k in (0, 1, 4, 6, 8, 12, 14) else vmem_spec for k in range(16)),
+        scratch_shapes=[
+            V((NG, 2, Q // 8, D), BF16), V((NG, 2, R, Q), BF16), V((2, 2, R // 2, C2), BF16),
+            V((2, 2, R // 2, C2), BF16), V((R, pair), F32), V((8 * NSP, 128), F32), V((T, D), BF16), V((T, D), F32),
+            V((R, F), F32), V((Q, D), F32), V((R, D), F32), V((R, D), F32),
+            pltpu.SemaphoreType.DMA((8,)), pltpu.SemaphoreType.DMA((8,)),
+        ],
+        compiler_params=pltpu.CompilerParams(vmem_limit_bytes=64000000),
         name="finish",
     )(*held)
 
@@ -894,6 +1034,7 @@
         and width == H * HD
         and width % (32 * n_sp) == 0
         and ff % (128 * n_sp) == 0
+        and width % 128 == 0
         and sum(count for _, count in vec_rows(width, ff, 2 * HD)[0].values()) <= 8 * n_sp
     )
 

time: 132 us -> 109 us (0.83)
  Pallas kernels: 123 us -> 108 us
  local copies, waits for them, and re-layouts: 7.62 us -> 0 us
    pallas_call x1, Pallas kernels: 120 us -> 104 us  [fused_local(): pl.pallas_call(functools.partial(fused_kernel, dims), out_shape=(shape((N...]
    unnamed x16 -> x0, local copies, waits for them, and re-layouts: 7.62 us -> none
    pallas_call x1, Pallas kernels: 2.23 us -> 3.89 us  [fused_local(): pl.pallas_call(functools.partial(finish_kernel, dims), out_shape=(shape((...]
where the time goes in v2:
time: 109 us
  Pallas kernels  108 us (99%)
    pallas_call x1, Pallas kernels, fused_local(): pl.pallas_call(functools.partial(fused_kernel, dims), out_shape=(shape((N...  104 us
    pallas_call x1, Pallas kernels, fused_local(): pl.pallas_call(functools.partial(finish_kernel, dims), out_shape=(shape((...  3.89 us

profile of v2, /device:TPU:0, one launch (start us, length us, event | category | flops | bytes accessed | tf_op | source)
XLA Modules:
  0.0 108.8 jit_solution(1273301024367072256)
XLA Ops:
  0.7 104.1 %fused_layer.1 = (bf16[4,2,48,768]{3,2,1,0:T(8,128)(2,1)}, bf16[4,2,96,384]{3,2,1,0:T(8,128)(2,1)}, bf16[2,2,48,384]{3,2,1,0:T(8,128)(2,1)}, bf16[2,2,48,384]{3,...) custom-call(bf16[256,768]{1,0:T(8,128)(2,1)} %x_h.1, ...), custom_call_target="tpu_custom_call" | custom-call | tf_op jit(solution)/shard_map/fused_layer/pallas_call | solution.py:980
  104.8 3.9 %finish.1 = (bf16[256,768]{1,0:T(8,128)(2,1)}, f32[256,768]{1,0:T(8,128)}, f32[768]{0:T(1024)}, f32[768]{0:T(1024)}, f32[96,768]{1,0:T(8,128)}, /*index=5*/f32[7...) custom-call(bf16[4,2,48,768]{3,2,1,0:T(8,128)(2,1)} %get-tuple-eleme, ...), custom_call_target="tpu_custom_call" | custom-call | tf_op jit(solution)/shard_map/finish/pallas_call | solution.py:1002

commit v3 on v2

--- a/solution.py
+++ b/solution.py
@@ -200,9 +200,9 @@
         ("wpx", NZ), ("wpy", NZ), ("wpz", NZ), ("wpg", NG),
         ("wpf", NZ), ("zfx", 1), ("zfy", 1),
         ("wfy", 2), ("wfx", 2), ("wfs", 2), ("wfz", NZ), ("wfg", 2 * NG),
-        ("ht", NZ), ("qg", 1), ("dk", NZ), ("dkv", NZ), ("kvg", 1),
-        ("wox", 1), ("woy", 1), ("woz", NZ), ("wog", NG),
-        ("wqy", 1), ("wqx", 1), ("wqz", NZ), ("wqg", NG),
+        ("ht", NZ), ("qg", H // 4), ("dk", NZ), ("dkv", NZ), ("kvg", 1),
+        ("wox", NZ), ("woy", NZ), ("woz", NZ), ("wog", NG),
+        ("wqy", H // 4), ("wqx", H // 4), ("wqz", NZ * (H // 4)), ("wqg", NG),
         ("wkv", NZ), ("vec", NSP), ("sm", NG), ("vg", NSP),
     ):
         take(name, n)
@@ -573,6 +573,98 @@
                     wf_g(o, core).start()
         l_fin.append(lc(fin_wf.at[pl.ds(pl.multiple_of(R * c, 16), R), :], o_wf.at[slot_wf, c]))
 
+    far_rx = pl.ds(pl.multiple_of(R // 2 * (1 - xx), 16), R // 2)
+    far_ry = pl.ds(pl.multiple_of(R // 2 * (1 - yy), 16), R // 2)
+    near_rx = pl.ds(pl.multiple_of(R // 2 * xx, 16), R // 2)
+    near_ry = pl.ds(pl.multiple_of(R // 2 * yy, 16), R // 2)
+    far_cy = pl.ds(pl.multiple_of(C2 * (1 - yy), 128), C2)
+    near_cy = pl.ds(pl.multiple_of(C2 * yy, 128), C2)
+    GC = 4 * HD
+
+    def owner_rows(k, core):
+        return pl.ds(pl.multiple_of(2 * R * k + R * core, 16), R)
+
+    def group_cols(m):
+        return pl.ds(GC * m, GC)
+
+    def side_cols(m, side):
+        return pl.ds(pl.multiple_of(GC * m + GC // 2 * side, 128), GC // 2)
+
+    def r_ht(k):
+        return rc("ht", k, oht.at[owner_rows(k, 1 - c), :], ht_r.at[k], partner)
+
+    def r_wox(k):
+        return rc("wox", k, wo_part.at[k, far_rx, :], rx_wo.at[k], xnb)
+
+    def r_woy(k):
+        return rc("woy", k, wo_s1.at[k, :, far_cy], ry_wo.at[k], ynb)
+
+    def r_woz(o):
+        return rc("woz", o, zs_wo.at[lax.rem(z + o, NZ)], rz_wo.at[o], z_peer(o))
+
+    def r_qg(m):
+        return rc("qg", m, qg2.at[own, group_cols(m)], qg2.at[other, group_cols(m)], partner)
+
+    def r_wqy(m):
+        return rc("wqy", m, wq_part.at[:, far_ry, group_cols(m)], ry_wq.at[:, :, group_cols(m)], ynb)
+
+    def r_wqx(m):
+        return rc("wqx", m, wq_s1.at[:, :, side_cols(m, 1 - xx)], rx_wq.at[m], xnb)
+
+    def r_wqz(o, m):
+        cols = pl.ds(GC // 2 * m, GC // 2)
+        return rc(
+            "wqz", NZ * m + o, zs_wq.at[lax.rem(z + o, NZ), :, cols], rz_wq.at[o, :, cols], z_peer(o)
+        )
+
+    def ht_send(k):
+        r_ht(k).start()
+
+    def wo_a(k):
+        r_ht(k).wait_recv()
+        total = mm(oht[owner_rows(k, c), :], og2[own, :]) + mm(ht_r[k], og2[other, :])
+        wo_part[k] = total.astype(BF16)
+        r_wox(k).start()
+
+    def wo_b(k):
+        r_wox(k).wait_recv()
+        wo_s1[k] = (wo_part[k, near_rx, :].astype(F32) + rx_wo[k].astype(F32)).astype(BF16)
+        r_woy(k).start()
+
+    def start_woz(o):
+        r_woz(o).start()
+
+    def wo_c(k):
+        r_woy(k).wait_recv()
+        zs_wo[k] = (wo_s1[k, :, near_cy].astype(F32) + ry_wo[k].astype(F32)).astype(BF16)
+        for o in range(1, NZ):
+            pl.when(lax.rem(z + o, NZ) == k)(functools.partial(start_woz, o))
+
+    def qg_send(m):
+        qg2[own, group_cols(m)] = qgt[group_cols(m), :].T
+        r_qg(m).start()
+
+    def wq_a(m):
+        r_qg(m).wait_recv()
+        for k in range(NZ):
+            wq_part[k, :, group_cols(m)] = mm(fit[owner_rows(k, c), :], qg2[:, group_cols(m)]).astype(BF16)
+        r_wqy(m).start()
+
+    def wq_b(m):
+        r_wqy(m).wait_recv()
+        cols = group_cols(m)
+        wq_s1[:, :, cols] = (wq_part[:, near_ry, cols].astype(F32) + ry_wq[:, :, cols].astype(F32)).astype(BF16)
+        r_wqx(m).start()
+
+    def wq_c(m):
+        r_wqx(m).wait_recv()
+        mine_cols = side_cols(m, xx)
+        zs_wq[:, :, GC // 2 * m : GC // 2 * (m + 1)] = (
+            wq_s1[:, :, mine_cols].astype(F32) + rx_wq[m].astype(F32)
+        ).astype(BF16)
+        for o in range(1, NZ):
+            r_wqz(o, m).start()
+
     def at_head(h):
         for when, what in EVENTS:
             pl.when(h == when)(functools.partial(run_event, what))
@@ -584,6 +676,21 @@
             "wp2": lambda: wp_first(2),
             "wp3": lambda: wp_first(3),
             "wp_second": wp_second,
+            "ht0": lambda: ht_send(0),
+            "ht1": lambda: ht_send(1),
+            "ht2": lambda: ht_send(2),
+            "woa0": lambda: wo_a(0),
+            "woa1": lambda: wo_a(1),
+            "woa2": lambda: wo_a(2),
+            "wob0": lambda: wo_b(0),
+            "wob1": lambda: wo_b(1),
+            "woc0": lambda: wo_c(0),
+            "qg0": lambda: qg_send(0),
+            "qg1": lambda: qg_send(1),
+            "wqa0": lambda: wq_a(0),
+            "wqa1": lambda: wq_a(1),
+            "wqb0": lambda: wq_b(0),
+            "wqc0": lambda: wq_c(0),
             "zf_first": zf_first,
             "zf_second": zf_second,
             "zf_third": zf_third,
@@ -647,14 +754,8 @@
         s_dk.append(rc("dk", k, dkv_b.at[block_rows(k, 1 - c), :], rdk.at[k], partner))
         send(s_dk[-1])
 
-    s_ht = []
-    for k in range(NZ):
-        rows = pl.ds(pl.multiple_of(2 * R * k + R * (1 - c), 16), R)
-        s_ht.append(rc("ht", k, oht.at[rows, :], ht_r.at[k], partner))
-        send(s_ht[-1])
-    qg2[own, :] = qgt[...].T
-    s_qg = rc("qg", 0, qg2.at[own], qg2.at[other], partner)
-    send(s_qg)
+    ht_send(3)
+    qg_send(2)
 
     for copy in s_dk:
         copy.wait_recv()
@@ -670,29 +771,11 @@
         for i in range(count):
             vec[at + i : at + i + 1, :] = row[:, 128 * i : 128 * (i + 1)]
 
-    for copy in s_ht:
-        copy.wait_recv()
-    for k in range(NZ):
-        rows = pl.ds(pl.multiple_of(2 * R * k + R * c, 16), R)
-        wo_part[k] = (mm(oht[rows, :], og2[own, :]) + mm(ht_r[k], og2[other, :])).astype(BF16)
-    far_rx = pl.ds(pl.multiple_of(R // 2 * (1 - xx), 16), R // 2)
-    far_ry = pl.ds(pl.multiple_of(R // 2 * (1 - yy), 16), R // 2)
-    near_rx = pl.ds(pl.multiple_of(R // 2 * xx, 16), R // 2)
-    near_ry = pl.ds(pl.multiple_of(R // 2 * yy, 16), R // 2)
-    far_cx = pl.ds(pl.multiple_of(C2 * (1 - xx), 128), C2)
-    far_cy = pl.ds(pl.multiple_of(C2 * (1 - yy), 128), C2)
-    near_cx = pl.ds(pl.multiple_of(C2 * xx, 128), C2)
-    near_cy = pl.ds(pl.multiple_of(C2 * yy, 128), C2)
-    s_wox = rc("wox", 0, wo_part.at[:, far_rx, :], rx_wo, xnb)
-    send(s_wox)
-    s_qg.wait_recv()
-    for k in range(NZ):
-        rows = pl.ds(pl.multiple_of(2 * R * k + R * c, 16), R)
-        wq_part[k] = mm(fit[rows, :], qg2[...]).astype(BF16)
-    s_wqy = rc("wqy", 0, wq_part.at[:, far_ry, :], ry_wq, ynb)
-    send(s_wqy)
-
-    zf_third()
+    wo_a(3)
+    wq_a(2)
+    wq_b(1)
+    wo_b(2)
+    wo_c(1)
 
     s_mlp.wait_recv()
     for i in range(T // 128):
@@ -702,28 +785,26 @@
         lo_v[rows, :] = ((x2[rows, :].astype(F32) + branch) + mlp).astype(BF16)
     l_lo = lc(lo_v, o_lo)
 
-    s_wox.wait_recv()
-    wo_s1[...] = (wo_part[:, near_rx, :].astype(F32) + rx_wo[...].astype(F32)).astype(BF16)
-    s_woy = rc("woy", 0, wo_s1.at[:, :, far_cy], ry_wo, ynb)
-    send(s_woy)
-    s_wqy.wait_recv()
-    wq_s1[...] = (wq_part[:, near_ry, :].astype(F32) + ry_wq[...].astype(F32)).astype(BF16)
-    s_wqx = rc("wqx", 0, wq_s1.at[:, :, far_cx], rx_wq, xnb)
-    send(s_wqx)
-
-    s_woy.wait_recv()
-    zs_wo[...] = (wo_s1[:, :, near_cy].astype(F32) + ry_wo[...].astype(F32)).astype(BF16)
-    s_woz = []
-    for o in range(1, NZ):
-        s_woz.append(rc("woz", o, zs_wo.at[lax.rem(z + o, NZ)], rz_wo.at[o], z_peer(o)))
-        send(s_woz[-1])
-    s_wqx.wait_recv()
-    zs_wq[...] = (wq_s1[:, :, near_cx].astype(F32) + rx_wq[...].astype(F32)).astype(BF16)
-    s_wqz = []
-    for o in range(1, NZ):
-        s_wqz.append(rc("wqz", o, zs_wq.at[lax.rem(z + o, NZ)], rz_wq.at[o], z_peer(o)))
-        send(s_wqz[-1])
-
+    zf_second()
+    wo_b(3)
+    wq_b(2)
+    wq_c(1)
+    wo_c(2)
+
+    s_sec.wait_recv()
+    sums = [jnp.zeros((1, D), F32) for _ in range(6)]
+    for i in range(T // 128):
+        rows = pl.ds(128 * i, 128)
+        ig_v[rows, :] = mm(qg2[rows, :], wq_v[...], NT)
+        second_grad = sec_all[rows, :] + sec_r[rows, :]
+        sec_all[rows, :] = second_grad * g2
+        up = og2[rows, :].astype(F32)
+        for k, value in enumerate((qg2[rows, :].astype(F32), up, second_grad * nrm[rows, :], second_grad)):
+            sums[2 + k] = sums[2 + k] + jnp.sum(value, axis=0, keepdims=True)
+
+    wo_c(3)
+    wq_c(2)
+    zf_third()
     wp_third()
     wf_fourth()
 
@@ -743,20 +824,14 @@
     send(s_kvg)
     put("b_keyval", jnp.sum(jnp.concatenate(kv_grads, axis=0).astype(F32), axis=0, keepdims=True))
 
-    s_sec.wait_recv()
-    sums = [jnp.zeros((1, D), F32) for _ in range(6)]
     for i in range(T // 128):
         rows = pl.ds(128 * i, 128)
-        first_grad = mm(qg2[rows, :], wq_v[...], NT) + mm(kv_grads[i], wkv_v[...], NT)
-        second_grad = sec_all[rows, :] + sec_r[rows, :]
+        first_grad = ig_v[rows, :] + mm(kv_grads[i], wkv_v[...], NT)
         n = nrm[rows, :]
-        up = og2[rows, :].astype(F32)
-        u = first_grad * g1 + second_grad * g2
+        u = first_grad * g1 + sec_all[rows, :]
         back = u - jnp.mean(u, axis=-1, keepdims=True) - n * jnp.mean(u * n, axis=-1, keepdims=True)
-        ig_v[rows, :] = up + inv[rows, 0:1] * back
-        for k, value in enumerate(
-            (first_grad * n, first_grad, qg2[rows, :].astype(F32), up, second_grad * n, second_grad)
-        ):
+        ig_v[rows, :] = og2[rows, :].astype(F32) + inv[rows, 0:1] * back
+        for k, value in enumerate((first_grad * n, first_grad)):
             sums[k] = sums[k] + jnp.sum(value, axis=0, keepdims=True)
     l_ig = lc(ig_v, o_ig)
     for name, row in zip(("ln1_gain", "ln1_bias", "b_query", "column", "ln2_gain", "ln2_bias"), sums):
@@ -795,7 +870,7 @@
 
     total = zs_wo[z].astype(F32)
     for o in range(1, NZ):
-        s_woz[o - 1].wait_recv()
+        r_woz(o).wait_recv()
         total = total + rz_wo[o].astype(F32)
     fin_wo[...] = total.astype(BF16)
     s_wog = [rc("wog", o, fin_wo, o_wo.at[xx, yy], xy_peer(o, c)) for o in range(1, NG)]
@@ -804,7 +879,8 @@
     l_fo = lc(fin_wo, o_wo.at[xx, yy])
     total = zs_wq[z].astype(F32)
     for o in range(1, NZ):
-        s_wqz[o - 1].wait_recv()
+        for m in range(H // 4):
+            r_wqz(o, m).wait_recv()
         total = total + rz_wq[o].astype(F32)
     fin_wq[...] = total.astype(BF16)
     s_wqg = [rc("wqg", o, fin_wq, o_wq.at[yy, xx], xy_peer(o, c)) for o in range(1, NG)]
@@ -843,6 +919,18 @@
         y_chunk(2 * (1 - yy) + k).wait_send()
         x_chunk(2 * k + 1 - xx).wait_send()
         wf_second_send(k).wait_send()
+    for k in range(NZ):
+        r_ht(k).wait_send()
+        r_wox(k).wait_send()
+        r_woy(k).wait_send()
+    for m in range(H // 4):
+        r_qg(m).wait_send()
+        r_wqy(m).wait_send()
+        r_wqx(m).wait_send()
+    for o in range(1, NZ):
+        r_woz(o).wait_send()
+        for m in range(H // 4):
+            r_wqz(o, m).wait_send()
     zf_x.wait_send()
     zf_y.wait_send()
     for o in range(1, NZ):
@@ -861,18 +949,32 @@
 
 EVENTS = (
     (0, "wp0"),
-    (1, "wf_first0"),
-    (1, "wf_first1"),
-    (1, "wp1"),
-    (2, "wf_second0"),
-    (3, "wp2"),
-    (5, "wf_second1"),
-    (5, "wp3"),
-    (6, "wf_third1"),
-    (7, "wp_second"),
-    (8, "wf_third0"),
-    (9, "zf_first"),
-    (11, "zf_second"),
+    (2, "wf_first0"),
+    (2, "wf_first1"),
+    (3, "wp1"),
+    (3, "ht0"),
+    (4, "woa0"),
+    (4, "qg0"),
+    (4, "wf_second0"),
+    (4, "wp2"),
+    (5, "wqa0"),
+    (6, "wf_second1"),
+    (6, "wp3"),
+    (6, "ht1"),
+    (7, "woa1"),
+    (8, "wf_third1"),
+    (8, "wp_second"),
+    (8, "qg1"),
+    (9, "wqa1"),
+    (9, "wob0"),
+    (9, "wqb0"),
+    (9, "ht2"),
+    (10, "wf_third0"),
+    (10, "woa2"),
+    (11, "zf_first"),
+    (11, "woc0"),
+    (11, "wqc0"),
+    (11, "wob1"),
 )
 
 
@@ -921,7 +1023,9 @@
             rows = slice(R // 2 * a, R // 2 * (a + 1))
             cols = slice(C2 * b, C2 * (b + 1))
             out_v[rows, cols] = wo[a, b].astype(F32)
-            query_v[rows, cols] = wq[a, b].astype(F32)
+            for m in range(H // 4):
+                at = 4 * HD * m + 2 * HD * b
+                query_v[rows, at : at + 2 * HD] = wq[a, b, :, 2 * HD * m : 2 * HD * (m + 1)].astype(F32)
     put_out(out_v, w_attn_out)
     put_out(query_v, w_query)
     arrive["wkv"].wait()
@@ -968,12 +1072,13 @@
         V((D, T), BF16), V((D, T), BF16), V((NZ, R, T), BF16), V((2 * T, D), BF16),
         V((NZ, R, D), BF16), V((NZ, R // 2, D), BF16), V((NZ, R // 2, D), BF16), V((NZ, R // 2, C2), BF16),
         V((NZ, R // 2, C2), BF16), V((NZ, R // 2, C2), BF16), V((R // 2, C2), BF16),
-        V((NZ, R, D), BF16), V((NZ, R // 2, D), BF16), V((NZ, R // 2, D), BF16), V((NZ, R // 2, C2), BF16),
+        V((NZ, R, D), BF16), V((NZ, R // 2, D), BF16), V((NZ, R // 2, D), BF16),
+        V((H // 4, NZ, R // 2, 2 * HD), BF16),
         V((NZ, R // 2, C2), BF16), V((NZ, R // 2, C2), BF16), V((R // 2, C2), BF16),
         V((8 * NSP, 128), F32), V((NSP, 8, 128), F32), V((NZ, R, pair), F32), V((NZ, R, pair), BF16),
         V((NZ, R, pair), BF16), V((NG, R + 8, 128), F32), V((R, 128), F32), V((8, 128), F32),
         V((T, D), BF16), V((T, D), F32), V((T, pair), F32), V((T, pair), F32), V((8, T), F32), V((8, T), F32),
-        pltpu.SemaphoreType.DMA((40,)), pltpu.SemaphoreType.DMA((128,)), pltpu.SemaphoreType.DMA((128,)),
+        pltpu.SemaphoreType.DMA((40,)), pltpu.SemaphoreType.DMA((160,)), pltpu.SemaphoreType.DMA((160,)),
     ]
     any_spec = pl.BlockSpec(memory_space=pl.ANY)
     shape = jax.ShapeDtypeStruct

time: 109 us -> 106 us (0.972)
  Pallas kernels: 108 us -> 105 us
    pallas_call x1, Pallas kernels: 104 us -> 101 us  [fused_local(): pl.pallas_call(functools.partial(fused_kernel, dims), out_shape=(shape((N...]
where the time goes in v3:
time: 106 us
  Pallas kernels  105 us (99%)
    pallas_call x1, Pallas kernels, fused_local(): pl.pallas_call(functools.partial(fused_kernel, dims), out_shape=(shape((N...  101 us
    pallas_call x1, Pallas kernels, fused_local(): pl.pallas_call(functools.partial(finish_kernel, dims), out_shape=(shape((...  3.89 us

profile of v3, /device:TPU:0, one launch (start us, length us, event | category | flops | bytes accessed | tf_op | source)
XLA Modules:
  0.0 106.0 jit_solution(10862014043266122694)
XLA Ops:
  0.7 101.3 %fused_layer.1 = (bf16[4,2,48,768]{3,2,1,0:T(8,128)(2,1)}, bf16[4,2,96,384]{3,2,1,0:T(8,128)(2,1)}, bf16[2,2,48,384]{3,2,1,0:T(8,128)(2,1)}, bf16[2,2,48,384]{3,...) custom-call(bf16[256,768]{1,0:T(8,128)(2,1)} %x_h.1, ...), custom_call_target="tpu_custom_call" | custom-call | tf_op jit(solution)/shard_map/fused_layer/pallas_call | solution.py:1085
  102.0 3.9 %finish.1 = (bf16[256,768]{1,0:T(8,128)(2,1)}, f32[256,768]{1,0:T(8,128)}, f32[768]{0:T(1024)}, f32[768]{0:T(1024)}, f32[96,768]{1,0:T(8,128)}, /*index=5*/f32[7...) custom-call(bf16[4,2,48,768]{3,2,1,0:T(8,128)(2,1)} %get-tuple-eleme, ...), custom_call_target="tpu_custom_call" | custom-call | tf_op jit(solution)/shard_map/finish/pallas_call | solution.py:1107

commit v4 on v3

--- a/solution.py
+++ b/solution.py
@@ -98,6 +98,7 @@
     zs_wp,
     rz_wp,
     rzf,
+    zf_pair,
     zf_s0,
     rx_zf,
     zf_s1,
@@ -188,6 +189,14 @@
     def xy_peer(o, core):
         return (lax.rem(g + o, NG), 2 * z + core)
 
+    def block_rows(k, core):
+        return pl.ds(pl.multiple_of((2 * k + core) * T, T), T)
+
+    mate = z + 1 - 2 * lax.rem(z, 2)
+    far = 2 * (1 - lax.div(z, 2))
+    outer = jnp.logical_or(z == 0, z == NZ - 1)
+    to_mate = (g, 2 * mate + c)
+
     base = {}
     used = [0]
 
@@ -196,9 +205,9 @@
         used[0] += n
 
     for name, n in (
-        ("x", 1), ("og", 1), ("kv", NSP), ("mlp", 1), ("sec", 1),
+        ("x", 1), ("og", 1), ("kv", NZ), ("kvp", NZ), ("mlp", 1), ("sec", 1),
         ("wpx", NZ), ("wpy", NZ), ("wpz", NZ), ("wpg", NG),
-        ("wpf", NZ), ("zfx", 1), ("zfy", 1),
+        ("wpf", 5), ("zfx", 1), ("zfy", 1),
         ("wfy", 2), ("wfx", 2), ("wfs", 2), ("wfz", NZ), ("wfg", 2 * NG),
         ("ht", NZ), ("qg", H // 4), ("dk", NZ), ("dkv", NZ), ("kvg", 1),
         ("wox", NZ), ("woy", NZ), ("woz", NZ), ("wog", NG),
@@ -241,6 +250,11 @@
         far_y = lax.div(j, 2) == 0
         far_x = lax.rem(j, 2) == 0
         return 2 * jnp.where(far_y, 1 - yy, yy) + jnp.where(far_x, xx, 1 - xx)
+
+    def chunk_y(j):
+        far_y = lax.div(j, 2) == 0
+        far_x = lax.rem(j, 2) == 0
+        return 2 * jnp.where(far_y, yy, 1 - yy) + jnp.where(far_x, xx, 1 - xx)
 
     own = pl.ds(0, T)
     other = pl.ds(T, T)
@@ -332,10 +346,13 @@
         kv = mm(fi2[rows, :], wkv_v[...]) + bkv_v[...]
         kv = jnp.where(lanes < HD, turn(kv, rows, 1.0), kv)
         kv_all[pl.ds(pl.multiple_of(d * T + 128 * i, 128), 128), :] = kv.astype(BF16)
-    mine = pl.ds(pl.multiple_of(d * T, T), T)
-    s_kv = [rc("kv", o, kv_all.at[mine], kv_all.at[mine], sp_peer(o)) for o in range(1, NSP)]
+    mine = kv_all.at[block_rows(z, c)]
+    s_kv = [rc("kv", o, mine, mine, z_peer(o)) for o in range(1, NZ)]
     for copy in s_kv:
         send(copy)
+
+    def kv_pass(k):
+        return rc("kvp", k, kv_all.at[block_rows(k, c)], kv_all.at[block_rows(k, c)], partner)
 
     s_x.wait_recv()
     norms(T, False)
@@ -351,9 +368,13 @@
         far = pl.ds(pl.multiple_of(QH // 2 * (1 - xx), 16), QH // 2)
         return rc("wpx", q, wp_part.at[q, far, :], rx_wp.at[q], xnb)
 
-    def z_half(o):
-        q = lax.rem(z + o, NZ)
-        return rc("wpf", o, wp_part.at[q, pl.ds(QH, QH), :], rzf.at[o], z_peer(o))
+    def z_half(q, slot):
+        return rc("wpf", slot, wp_part.at[q, pl.ds(QH, QH), :], rzf.at[slot], to_mate)
+
+    def z_pair(side):
+        return rc("wpf", 3 + side, zf_pair.at[side], rzf.at[3], (g, 2 * (far + side) + c))
+
+    z_got = rc("wpf", 3 + lax.rem(z, 2), zf_pair.at[0], rzf.at[3], (g, 2 * far + c))
 
     def y_chunk(q):
         side = lax.rem(q, 2)
@@ -362,9 +383,6 @@
     def x_chunk(q):
         side = lax.div(q, 2)
         return rc("wfx", side, wf_part.at[q, pl.ds(D2, D2), :], rx_wf.at[side], xnb)
-
-    def start_z_half(o):
-        z_half(o).start()
 
     def mlp_chunk(j, carry):
         q = chunk_of(j)
@@ -385,8 +403,15 @@
             cols = pl.ds(128 * i, 128)
             wp_part[q, cols, :] = mm(act_s[q, :, cols], og2[...], TN).astype(BF16)
         x_half(q).start()
-        for o in range(1, NZ):
-            pl.when(lax.rem(z + o, NZ) == q)(functools.partial(start_z_half, o))
+
+        @pl.when(q == mate)
+        def _():
+            z_half(q, 0).start()
+
+        @pl.when(jnp.logical_and(outer, lax.div(q, 2) != lax.div(z, 2)))
+        def _():
+            z_half(q, 1 + lax.rem(q, 2)).start()
+
         for i in range(D // 128):
             rows = pl.ds(128 * i, 128)
             wf_part[q, rows, :] = mm(sit[rows, :], hg_s[q]).astype(BF16)
@@ -405,6 +430,10 @@
         return carry
 
     lax.fori_loop(0, NZ, mlp_chunk, 0)
+    for copy in s_kv:
+        copy.wait_recv()
+    for k in range(NZ):
+        send(kv_pass(k))
 
     def mlp_sums(i, carry):
         at = lax.rem(i + T // 128, 2 * T // 128) * 128
@@ -446,8 +475,8 @@
         key_pos = order_s[0, j] * block + row_in
         bias[pl.ds(block * j, block), :] = jnp.where(key_pos <= query_pos, 0.0, masked_score)
 
-    for copy in s_kv:
-        copy.wait_recv()
+    for k in range(NZ):
+        kv_pass(k).wait_recv()
     for j in range(S // 256):
         rows = pl.ds(256 * j, 256)
         kvt[:, rows] = kv_all[rows, :].T
@@ -469,12 +498,15 @@
     def wp_z(o):
         return rc("wpz", o, zs_wp.at[lax.rem(z + o, NZ)], rz_wp.at[o], z_peer(o))
 
-    def wp_second():
-        for q in range(NZ):
-            wp_y(q).wait_recv()
-            zs_wp[q] = (wp_s1[q, near_y, :].astype(F32) + ry_wp[q].astype(F32)).astype(BF16)
+    def start_wp_z(o):
+        wp_z(o).start()
+
+    def wp_second(j):
+        q = chunk_y(j)
+        wp_y(q).wait_recv()
+        zs_wp[q] = (wp_s1[q, near_y, :].astype(F32) + ry_wp[q].astype(F32)).astype(BF16)
         for o in range(1, NZ):
-            wp_z(o).start()
+            pl.when(lax.rem(z + o, NZ) == q)(functools.partial(start_wp_z, o))
 
     slot_wp = 2 * xx + yy
 
@@ -487,11 +519,20 @@
     zf_x = rc("zfx", 0, zf_s0.at[far_zx, :], rx_zf, xnb)
     zf_y = rc("zfy", 0, zf_s1.at[far_y, :], ry_zf, ynb)
 
+    def zf_mid():
+        @pl.when(jnp.logical_not(outer))
+        def _():
+            for side in range(2):
+                z_half(far + side, 1 + side).wait_recv()
+                total = wp_part[far + side, QH:, :].astype(F32) + rzf[1 + side].astype(F32)
+                zf_pair[side] = total.astype(BF16)
+                z_pair(side).start()
+
     def zf_first():
         total = wp_part[z, QH:, :].astype(F32)
-        for o in range(1, NZ):
-            z_half(o).wait_recv()
-            total = total + rzf[o].astype(F32)
+        z_half(mate, 0).wait_recv()
+        z_got.wait_recv()
+        total = total + rzf[0].astype(F32) + rzf[3].astype(F32)
         zf_s0[...] = total.astype(BF16)
         zf_x.start()
 
@@ -675,7 +716,11 @@
             "wp1": lambda: wp_first(1),
             "wp2": lambda: wp_first(2),
             "wp3": lambda: wp_first(3),
-            "wp_second": wp_second,
+            "wpy0": lambda: wp_second(0),
+            "wpy1": lambda: wp_second(1),
+            "wpy2": lambda: wp_second(2),
+            "wpy3": lambda: wp_second(3),
+            "zf_mid": zf_mid,
             "ht0": lambda: ht_send(0),
             "ht1": lambda: ht_send(1),
             "ht2": lambda: ht_send(2),
@@ -745,9 +790,6 @@
 
     lax.fori_loop(0, H, head, 0)
 
-    def block_rows(k, core):
-        return pl.ds(pl.multiple_of((2 * k + core) * T, T), T)
-
     dkv_b[...] = dkv[...].astype(BF16)
     s_dk = []
     for k in range(NZ):
@@ -784,12 +826,6 @@
         mlp = (mlp_all[rows, :] + mlp_r[rows, :]) + vecs[6:7, :]
         lo_v[rows, :] = ((x2[rows, :].astype(F32) + branch) + mlp).astype(BF16)
     l_lo = lc(lo_v, o_lo)
-
-    zf_second()
-    wo_b(3)
-    wq_b(2)
-    wq_c(1)
-    wo_c(2)
 
     s_sec.wait_recv()
     sums = [jnp.zeros((1, D), F32) for _ in range(6)]
@@ -802,11 +838,11 @@
         for k, value in enumerate((qg2[rows, :].astype(F32), up, second_grad * nrm[rows, :], second_grad)):
             sums[2 + k] = sums[2 + k] + jnp.sum(value, axis=0, keepdims=True)
 
-    wo_c(3)
-    wq_c(2)
-    zf_third()
-    wp_third()
-    wf_fourth()
+    wo_b(3)
+    wq_b(2)
+    zf_second()
+    wq_c(1)
+    wo_c(2)
 
     l_kvg.wait()
     for copy in s_dkv:
@@ -851,6 +887,12 @@
     for o in range(1, NZ):
         s_wkv.append(rc("wkv", o, wkv_b.at[lax.rem(z + o, NZ)], rkv.at[o], z_peer(o)))
         send(s_wkv[-1])
+
+    wo_c(3)
+    wq_c(2)
+    zf_third()
+    wp_third()
+    wf_fourth()
 
     for copy in s_wkv:
         copy.wait_recv()
@@ -931,10 +973,21 @@
         r_woz(o).wait_send()
         for m in range(H // 4):
             r_wqz(o, m).wait_send()
+    z_half(mate, 0).wait_send()
+
+    @pl.when(outer)
+    def _():
+        for side in range(2):
+            z_half(far + side, 1 + side).wait_send()
+
+    @pl.when(jnp.logical_not(outer))
+    def _():
+        for side in range(2):
+            z_pair(side).wait_send()
+
     zf_x.wait_send()
     zf_y.wait_send()
     for o in range(1, NZ):
-        z_half(o).wait_send()
         wp_z(o).wait_send()
         wf_z(o).wait_send()
     for o in range(1, NG):
@@ -949,29 +1002,33 @@
 
 EVENTS = (
     (0, "wp0"),
-    (2, "wf_first0"),
+    (1, "wf_first0"),
     (2, "wf_first1"),
-    (3, "wp1"),
-    (3, "ht0"),
-    (4, "woa0"),
-    (4, "qg0"),
-    (4, "wf_second0"),
+    (2, "wp1"),
+    (3, "zf_mid"),
+    (3, "wf_second0"),
     (4, "wp2"),
-    (5, "wqa0"),
+    (4, "ht0"),
+    (5, "wpy0"),
+    (5, "woa0"),
+    (5, "qg0"),
     (6, "wf_second1"),
     (6, "wp3"),
-    (6, "ht1"),
-    (7, "woa1"),
-    (8, "wf_third1"),
-    (8, "wp_second"),
+    (6, "wqa0"),
+    (7, "wpy1"),
+    (7, "wpy2"),
+    (7, "wf_third1"),
+    (7, "ht1"),
+    (8, "wpy3"),
+    (8, "woa1"),
     (8, "qg1"),
+    (9, "wf_third0"),
     (9, "wqa1"),
     (9, "wob0"),
     (9, "wqb0"),
     (9, "ht2"),
-    (10, "wf_third0"),
     (10, "woa2"),
-    (11, "zf_first"),
+    (10, "zf_first"),
     (11, "woc0"),
     (11, "wqc0"),
     (11, "wob1"),
@@ -1062,7 +1119,8 @@
         V((T, pair), BF16), V((NZ, 2 * T, Q), BF16), V((NZ, 2 * T, Q), BF16),
         V((2 * T, D), F32), V((2 * T, D), F32), V((T, D), F32), V((T, D), F32),
         V((NZ, Q, D), BF16), V((NZ, Q // 4, D), BF16), V((NZ, Q // 4, D), BF16), V((NZ, Q // 8, D), BF16),
-        V((NZ, Q // 8, D), BF16), V((NZ, Q // 8, D), BF16), V((NZ, Q // 2, D), BF16), V((Q // 2, D), BF16),
+        V((NZ, Q // 8, D), BF16), V((NZ, Q // 8, D), BF16), V((NZ, Q // 2, D), BF16), V((2, Q // 2, D), BF16),
+        V((Q // 2, D), BF16),
         V((Q // 4, D), BF16), V((Q // 4, D), BF16), V((Q // 8, D), BF16), V((2, Q // 8, D), BF16),
         V((NZ, D, Q), BF16), V((2, D // 2, Q), BF16), V((2, D // 2, Q), BF16), V((2, D // 2, Q), BF16),
         V((2, D // 2, Q), BF16), V((2, D // 2, Q), BF16), V((D, Q), BF16), V((NZ, 2 * R, Q), BF16), V((2 * R, Q), BF16),

time: 106 us -> 107 us (level); the launches traced: 106 us -> 105 us
  no operation moved by 1% of the time
where the time goes in v4:
time: 107 us; the launch traced here: 105 us
  Pallas kernels  105 us (98%)
    pallas_call x1, Pallas kernels, fused_local(): pl.pallas_call(functools.partial(fused_kernel, dims), out_shape=(shape((N...  101 us
    pallas_call x1, Pallas kernels, fused_local(): pl.pallas_call(functools.partial(finish_kernel, dims), out_shape=(shape((...  3.89 us

profile of v4, /device:TPU:0, one launch (start us, length us, event | category | flops | bytes accessed | tf_op | source)
XLA Modules:
  0.0 105.3 jit_solution(11048672116940308904)
XLA Ops:
  0.7 100.6 %fused_layer.1 = (bf16[4,2,48,768]{3,2,1,0:T(8,128)(2,1)}, bf16[4,2,96,384]{3,2,1,0:T(8,128)(2,1)}, bf16[2,2,48,384]{3,2,1,0:T(8,128)(2,1)}, bf16[2,2,48,384]{3,...) custom-call(bf16[256,768]{1,0:T(8,128)(2,1)} %x_h.1, ...), custom_call_target="tpu_custom_call" | custom-call | tf_op jit(solution)/shard_map/fused_layer/pallas_call | solution.py:1143
  101.3 3.9 %finish.1 = (bf16[256,768]{1,0:T(8,128)(2,1)}, f32[256,768]{1,0:T(8,128)}, f32[768]{0:T(1024)}, f32[768]{0:T(1024)}, f32[96,768]{1,0:T(8,128)}, /*index=5*/f32[7...) custom-call(bf16[4,2,48,768]{3,2,1,0:T(8,128)(2,1)} %get-tuple-eleme, ...), custom_call_target="tpu_custom_call" | custom-call | tf_op jit(solution)/shard_map/finish/pallas_call | solution.py:1165

commit v5 on v4

--- a/solution.py
+++ b/solution.py
@@ -827,6 +827,13 @@
         lo_v[rows, :] = ((x2[rows, :].astype(F32) + branch) + mlp).astype(BF16)
     l_lo = lc(lo_v, o_lo)
 
+    zf_second()
+    wo_b(3)
+    wq_b(2)
+    wf_fourth()
+    zf_third()
+    wp_third()
+
     s_sec.wait_recv()
     sums = [jnp.zeros((1, D), F32) for _ in range(6)]
     for i in range(T // 128):
@@ -838,9 +845,6 @@
         for k, value in enumerate((qg2[rows, :].astype(F32), up, second_grad * nrm[rows, :], second_grad)):
             sums[2 + k] = sums[2 + k] + jnp.sum(value, axis=0, keepdims=True)
 
-    wo_b(3)
-    wq_b(2)
-    zf_second()
     wq_c(1)
     wo_c(2)
 
@@ -890,9 +894,6 @@
 
     wo_c(3)
     wq_c(2)
-    zf_third()
-    wp_third()
-    wf_fourth()
 
     for copy in s_wkv:
         copy.wait_recv()

time: 107 us -> 100 us (0.935)
  Pallas kernels: 105 us -> 98.6 us
    pallas_call x1, Pallas kernels: 101 us -> 94.7 us  [fused_local(): pl.pallas_call(functools.partial(fused_kernel, dims), out_shape=(shape((N...]
where the time goes in v5:
time: 100 us; the launch traced here: 99.4 us
  Pallas kernels  98.6 us (99%)
    pallas_call x1, Pallas kernels, fused_local(): pl.pallas_call(functools.partial(fused_kernel, dims), out_shape=(shape((N...  94.7 us
    pallas_call x1, Pallas kernels, fused_local(): pl.pallas_call(functools.partial(finish_kernel, dims), out_shape=(shape((...  3.89 us

profile of v5, /device:TPU:0, one launch (start us, length us, event | category | flops | bytes accessed | tf_op | source)
XLA Modules:
  0.0 99.4 jit_solution(2447808424017582221)
XLA Ops:
  0.7 94.7 %fused_layer.1 = (bf16[4,2,48,768]{3,2,1,0:T(8,128)(2,1)}, bf16[4,2,96,384]{3,2,1,0:T(8,128)(2,1)}, bf16[2,2,48,384]{3,2,1,0:T(8,128)(2,1)}, bf16[2,2,48,384]{3,...) custom-call(bf16[256,768]{1,0:T(8,128)(2,1)} %x_h.1, ...), custom_call_target="tpu_custom_call" | custom-call | tf_op jit(solution)/shard_map/fused_layer/pallas_call | solution.py:1144
  95.3 3.9 %finish.1 = (bf16[256,768]{1,0:T(8,128)(2,1)}, f32[256,768]{1,0:T(8,128)}, f32[768]{0:T(1024)}, f32[768]{0:T(1024)}, f32[96,768]{1,0:T(8,128)}, /*index=5*/f32[7...) custom-call(bf16[4,2,48,768]{3,2,1,0:T(8,128)(2,1)} %get-tuple-eleme, ...), custom_call_target="tpu_custom_call" | custom-call | tf_op jit(solution)/shard_map/finish/pallas_call | solution.py:1166
